TPU v7x, 32 devices: a whole 2x2x4 slice. The times are simulated.
32 devices in a mesh: gz: 2 (over core), row: 4 (over y, x), col: 4 (over z).
Axes of the slice: x: 2, y: 2, z: 4, core: 2. Of those that a mesh axis runs over, the one named last changes fastest.
Arguments:
- right_sides: float32 [32, 4, 16, 256], P(('gz', 'row', 'col')), may hold values from -6 to 6
- lower_inverse: bfloat16 [32, 4, 256, 256], P(('gz', 'row', 'col')), may hold values from -0.375 to 0.375
- upper_inverse: bfloat16 [32, 4, 256, 256], P(('gz', 'row', 'col')), may hold values from -0.375 to 0.375
- lower_blocks: bfloat16 [32, 4, 2, 256, 256], P(('gz', 'row', 'col')), may hold values from -0.125 to 0.125
- upper_blocks: bfloat16 [32, 4, 2, 256, 256], P(('gz', 'row', 'col')), may hold values from -0.125 to 0.125
- node_widths: int32 [32, 4], P(('gz', 'row', 'col')), may hold values from 128 to 256, as said below
- far_levels: int32 [32, 4], P(('gz', 'row', 'col')), may hold values from 0 to 5, as said below
- owner_level: int32 [32], replicated, may hold values from 0 to 5, as said below
Outputs:
- solution: float32 [32, 4, 16, 256], P(('gz', 'row', 'col'))
Inputs may be any that keep to these rules, and one draw needn't show every extreme that they name: Columns c >= node_widths of a supernode are padding; every device holds a supernode with all 256 columns. `far_levels`: between 2 and 5 where the supernode has two or more ancestors, but never past the root; 1 where it has one; 0 for the root and for the slot of the device that owns no separator. `owner_level`: every separator of level u is owned by exactly one device of its group (the devices t with the same t // 2**u); one device owns none and holds 0.
All inputs are finite; a program needn't handle non-finite values.
Results may differ from a plain program's by a relative error of at most 0.018.
Values may be sent and summed in bfloat16 or wider, within the bound.
A program may use at most 64 MiB of HBM per device.

v0:
```python
import functools

import jax
import jax.numpy as jnp
from jax import lax
from jax.experimental import pallas as pl
from jax.experimental.pallas import tpu as pltpu
from jax.sharding import PartitionSpec as P

W = 256
RHS = 16
NB = 2
LOCAL_LEVELS = 2
LOCAL_COUNT = 3
OWN = LOCAL_COUNT
AXES = ("gz", "row", "col")


def flip_bits(coord, mask):
    flipped = coord
    bit = 1
    while bit <= mask:
        if mask & bit:
            flipped = flipped + bit - 2 * bit * lax.rem(lax.div(coord, bit), 2)
        bit *= 2
    return flipped


def exchange_plan(level, low=0):
    phases = []
    while low < level:
        high = min(low + 4, level)
        phases.append([step << low for step in range((1 << (high - low)) - 1, 0, -1)])
        low = high
    return phases


def times(vectors, matrix):
    return lax.dot_general(
        vectors, matrix, (((1,), (1,)), ((), ())), preferred_element_type=jnp.float32
    )


def half(values):
    return values.astype(jnp.bfloat16)


HANDOUT = {
    2: ((1, False, 0),),
    3: ((2, False, 0),(1, False, 1)),
    4: ((2, False, 1),(1, True, 0)),
    5: ((1, True, 1),),
}
NEAR_BITS = 2
NEAR = 2**NEAR_BITS


def kernel(
    spans,
    plans,
    down_plans,
    rights_hbm,
    lower_inverse_hbm,
    upper_inverse_hbm,
    lower_blocks_hbm,
    upper_blocks_hbm,
    widths_ref,
    far_ref,
    owner_ref,
    out_ref,
    rights,
    lower_inverse,
    upper_inverse,
    lower_blocks,
    upper_blocks,
    outgoing,
    incoming,
    fused,
    replicas,
    fars,
    bases,
    load_sems,
    send_sems,
    recv_sems,
    bulk_send_sems,
    bulk_recv_sems,
):
    layer_span, row_span, col_span = spans
    upper_levels = len(plans)
    layer_at = lax.axis_index("gz")
    row_at = lax.axis_index("row")
    col_at = lax.axis_index("col")
    device = (layer_at * row_span + row_at) * col_span + col_at

    def peer(offset):
        return (
            flip_bits(layer_at, offset // (row_span * col_span)),
            flip_bits(row_at, offset // col_span % row_span),
            flip_bits(col_at, offset % col_span),
        )

    pieces = [
        (rights_hbm.at[0], rights),
        (lower_inverse_hbm.at[0, pl.ds(0, 2)], lower_inverse.at[pl.ds(0, 2)]),
        (lower_blocks_hbm.at[0, pl.ds(0, 2)], lower_blocks.at[pl.ds(0, 2)]),
        (lower_inverse_hbm.at[0, pl.ds(2, 2)], lower_inverse.at[pl.ds(2, 2)]),
        (lower_blocks_hbm.at[0, pl.ds(2, 2)], lower_blocks.at[pl.ds(2, 2)]),
        (upper_blocks_hbm.at[0], upper_blocks),
        (upper_inverse_hbm.at[0], upper_inverse),
    ]
    loads = [
        pltpu.make_async_copy(source, target, load_sems.at[at])
        for at, (source, target) in enumerate(pieces)
    ]
    for load in loads:
        load.start()

    barrier = pltpu.get_barrier_semaphore()
    partners = sorted({offset for plan in plans for phase in plan for offset in phase})
    for offset in partners:
        pl.semaphore_signal(
            barrier, inc=1, device_id=peer(offset), device_id_type=pl.DeviceIdType.MESH
        )

    columns = lax.broadcasted_iota(jnp.int32, (RHS, W), 1)

    def spread(scalar):
        return jnp.full((RHS, W), scalar, jnp.int32)

    inside = [columns < widths_ref[0, slot] for slot in range(LOCAL_COUNT + 1)]
    far = [spread(far_ref[0, slot]) for slot in range(LOCAL_COUNT + 1)]
    my_level = spread(owner_ref[device])
    zeros = jnp.zeros((RHS, W), jnp.float32)

    def padded(slot, values):
        return jnp.where(inside[slot], values, 0.0)

    counts = [0, 0]
    sends = []

    def launch(rounded, phase):
        outbox = counts[0]
        counts[0] += 1
        outgoing[outbox] = rounded
        copies = []
        for offset in phase:
            at = counts[1]
            counts[1] += 1
            copy = pltpu.make_async_remote_copy(
                src_ref=outgoing.at[outbox],
                dst_ref=incoming.at[at],
                send_sem=send_sems.at[at],
                recv_sem=recv_sems.at[at],
                device_id=peer(offset),
                device_id_type=pl.DeviceIdType.MESH,
            )
            copy.start()
            copies.append((copy, at))
        sends.extend(copies)
        return copies

    bulk = {}

    def hand_out(name, source, target, offset):
        at = len(bulk)
        bulk[name] = pltpu.make_async_remote_copy(
            src_ref=source,
            dst_ref=target,
            send_sem=bulk_send_sems.at[at],
            recv_sem=bulk_recv_sems.at[at],
            device_id=peer(offset),
            device_id_type=pl.DeviceIdType.MESH,
        )
        bulk[name].start()

    received = set()

    def await_bulk(name):
        if name not in received:
            received.add(name)
            bulk[name].wait_recv()

    def exchange(values, plan, narrow, beside):
        for index, phase in enumerate(plan):
            rounded = half(values)
            copies = launch(rounded, phase)
            if index == 0:
                beside()
            if narrow:
                values = rounded.astype(jnp.float32)
            for copy, at in copies:
                copy.wait_recv()
                values = values + incoming[at].astype(jnp.float32)
        return values

    pending = [None] + [zeros for _ in range(upper_levels)]

    def scatter_up(product, slot, height):
        for level in range(1, upper_levels + 1):
            pending[level] = pending[level] + jnp.where(
                far[slot] == level + LOCAL_LEVELS - 1 - height, product, 0.0
            )

    forward = [None] * (LOCAL_COUNT + 1)
    loads[0].wait()
    loads[1].wait()
    for slot in range(2):
        forward[slot] = padded(slot, times(half(rights[slot]), lower_inverse[slot]))
    loads[2].wait()
    near = times(half(forward[0]), lower_blocks[0, 0]) + times(
        half(forward[1]), lower_blocks[1, 0]
    )
    for slot in range(2):
        scatter_up(times(half(forward[slot]), lower_blocks[slot, 1]), slot, 0)
    loads[3].wait()
    loads[4].wait()
    forward[2] = padded(2, times(half(rights[2] - near), lower_inverse[2]))
    pending[1] = pending[1] + times(half(forward[2]), lower_blocks[2, 0])
    scatter_up(times(half(forward[2]), lower_blocks[2, 1]), 2, 1)

    pl.semaphore_wait(barrier, len(partners))

    wide_columns = lax.broadcasted_iota(jnp.int32, (W, W), 1)

    def lower_product(block_id):
        kept = jnp.where(
            wide_columns < widths_ref[0, OWN],
            lower_blocks[OWN, block_id].astype(jnp.float32),
            0.0,
        )
        return jnp.dot(half(kept), lower_inverse[OWN], preferred_element_type=jnp.float32)

    def upper_product(slot, block_id):
        return jnp.dot(
            upper_inverse[slot], upper_blocks[slot, block_id], preferred_element_type=jnp.float32
        )

    def split_times(values, matrix):
        large = half(values)
        small = half(values - large.astype(jnp.float32))
        return times(large, matrix) + times(small, matrix)

    far_is_near = jnp.full((W, W), far_ref[0, OWN], jnp.int32) == 1

    own_forward = [zeros]
    residue = [None]

    def own_solve(level):
        solved = padded(OWN, times(residue[0], lower_inverse[OWN]))
        own_forward[0] = own_forward[0] + jnp.where(my_level == level, solved, 0.0)

    def far_up(level):
        product = jnp.where(my_level == level, times(residue[0], fused[1]), 0.0)
        for target in range(level + 2, upper_levels + 1):
            pending[target] = pending[target] + jnp.where(
                far[OWN] == target - level, product, 0.0
            )

    wide_rows = lax.broadcasted_iota(jnp.int32, (W, W), 0)

    def upper_kept(block_id):
        return jnp.where(
            wide_rows < widths_ref[0, OWN], upper_product(OWN, block_id), 0.0
        )

    def beside_up(level):
        if level == 1:
            fars[0] = far[OWN].astype(jnp.float32)
            for offset in range(1, NEAR):
                hand_out(("far", offset), fars.at[0], fars.at[offset], offset)
            far_product = lower_product(1)
            fused[1] = half(far_product)
            fused[0] = half(lower_product(0) + jnp.where(far_is_near, far_product, 0.0))
            loads[5].wait()
            loads[6].wait()
            far_product = upper_kept(1)
            replicas[0, 1] = half(far_product)
            replicas[0, 0] = half(upper_kept(0) + jnp.where(far_is_near, far_product, 0.0))
        else:
            far_up(level - 1)
            own_solve(level - 1)
        if level == upper_levels:
            bases[0] = padded(OWN, split_times(own_forward[0], upper_inverse[OWN]))
            for offset in reversed(range(1, NEAR)):
                hand_out(("base", offset), bases.at[0], bases.at[offset], offset)
        for offset, relayed, block_id in HANDOUT.get(level, ()):
            kept = 2 if relayed else 0
            if relayed:
                await_bulk((2, False, block_id))
            hand_out(
                (offset, relayed, block_id),
                replicas.at[kept, block_id],
                replicas.at[kept + offset, block_id],
                offset,
            )
        if 3 <= level < 3 + LOCAL_COUNT:
            slot = level - 3
            for block_id in range(NB):
                fused[4 + 2 * slot + block_id] = half(upper_product(slot, block_id))

    for level in range(1, upper_levels + 1):
        gathered = exchange(
            pending[level], plans[level - 1], False, functools.partial(beside_up, level)
        )
        residue[0] = half(rights[OWN] - gathered)
        if level < upper_levels:
            product = times(residue[0], fused[0])
            pending[level + 1] = pending[level + 1] + jnp.where(my_level == level, product, 0.0)
    own_solve(upper_levels)

    known = [None] * (upper_levels + 1)

    def pick(slot, below, lowest):
        chosen = zeros
        for level in range(lowest, upper_levels + 1):
            chosen = chosen + jnp.where(far[slot] == level - below, known[level], 0.0)
        return half(chosen)

    own_solution = zeros
    leaf_base = [None] * LOCAL_COUNT
    far_part = [zeros]
    near_levels = [owner_ref[flip_bits(device, offset)] for offset in range(NEAR)]

    def holder(level):
        offset_of = jnp.int32(0)
        found = jnp.int32(0)
        for offset in range(min(NEAR, 2**level)):
            offset_of = jnp.where(near_levels[offset] == level, offset, offset_of)
            found = jnp.where(near_levels[offset] == level, 1, found)
        return offset_of, found

    def prepare(level):
        if level < 1 or level + 2 > upper_levels:
            return
        at, _ = holder(level)
        reach = fars[at]
        chosen = zeros
        for target in range(level + 2, upper_levels + 1):
            chosen = chosen + jnp.where(reach == float(target - level), known[target], 0.0)
        far_part[0] = times(half(chosen), replicas[at, 1])

    def beside_down(level):
        if level == upper_levels:
            for slot in range(LOCAL_COUNT):
                leaf_base[slot] = split_times(forward[slot], upper_inverse[slot])
        else:
            prepare(level - 1)

    for level in range(upper_levels, 0, -1):
        if level == upper_levels:
            solved = padded(OWN, split_times(own_forward[0], upper_inverse[OWN]))
            solved = jnp.where(my_level == level, solved, 0.0)
        else:
            at, found = holder(level)
            solved = bases[at] - far_part[0] - times(half(known[level + 1]), replicas[at, 0])
            solved = jnp.where(spread(found) == 1, solved, 0.0)
        own_solution = own_solution + jnp.where(my_level == level, solved, 0.0)
        if down_plans[level - 1]:
            known[level] = exchange(
                solved, down_plans[level - 1], True, functools.partial(beside_down, level)
            )
        else:
            known[level] = half(solved).astype(jnp.float32)
            beside_down(level)
        if level == upper_levels:
            for name in bulk:
                await_bulk(name)
    leaf_base[2] = leaf_base[2] - times(pick(2, 0, 2), fused[4 + 2 * 2 + 1])
    out_ref[0, OWN] = own_solution

    nearest = half(known[1])
    root = padded(2, leaf_base[2] - times(nearest, fused[4 + 2 * 2]))
    out_ref[0, 2] = root
    for slot in range(2):
        solved = leaf_base[slot] - times(pick(slot, -1, 1), fused[4 + 2 * slot + 1])
        solved = solved - times(half(root), fused[4 + 2 * slot])
        out_ref[0, slot] = padded(slot, solved)

    for copy, _ in sends:
        copy.wait_send()
    for copy in bulk.values():
        copy.wait_send()


def local(
    spans,
    right_sides,
    lower_inverse,
    upper_inverse,
    lower_blocks,
    upper_blocks,
    node_widths,
    far_levels,
    owner_level,
):
    layer_span, row_span, col_span = spans
    upper_levels = (layer_span * row_span * col_span).bit_length() - 1
    plans = [exchange_plan(level) for level in range(1, upper_levels + 1)]
    down_plans = [exchange_plan(level, NEAR_BITS) for level in range(1, upper_levels)]
    down_plans.append(plans[-1])
    phases = sum(len(plan) for plan in plans + down_plans)
    messages = sum(len(phase) for plan in plans + down_plans for phase in plan)
    handed = 2 * (NEAR - 1) + sum(len(row) for row in HANDOUT.values())
    hbm = pl.BlockSpec(memory_space=pl.ANY)
    smem = pl.BlockSpec(memory_space=pltpu.SMEM)
    return pl.pallas_call(
        functools.partial(kernel, spans, plans, down_plans),
        out_shape=jax.ShapeDtypeStruct(right_sides.shape, jnp.float32),
        in_specs=[hbm] * 5 + [smem] * 3,
        out_specs=pl.BlockSpec(memory_space=pltpu.VMEM),
        scratch_shapes=[
            pltpu.VMEM(right_sides.shape[1:], jnp.float32),
            pltpu.VMEM(lower_inverse.shape[1:], jnp.bfloat16),
            pltpu.VMEM(upper_inverse.shape[1:], jnp.bfloat16),
            pltpu.VMEM(lower_blocks.shape[1:], jnp.bfloat16),
            pltpu.VMEM(upper_blocks.shape[1:], jnp.bfloat16),
            pltpu.VMEM((phases, RHS, W), jnp.bfloat16),
            pltpu.VMEM((messages, RHS, W), jnp.bfloat16),
            pltpu.VMEM((4 + NB * LOCAL_COUNT, W, W), jnp.bfloat16),
            pltpu.VMEM((NEAR, NB, W, W), jnp.bfloat16),
            pltpu.VMEM((NEAR, RHS, W), jnp.float32),
            pltpu.VMEM((NEAR, RHS, W), jnp.float32),
            pltpu.SemaphoreType.DMA((7,)),
            pltpu.SemaphoreType.DMA((messages,)),
            pltpu.SemaphoreType.DMA((messages,)),
            pltpu.SemaphoreType.DMA((handed,)),
            pltpu.SemaphoreType.DMA((handed,)),
        ],
        compiler_params=pltpu.CompilerParams(collective_id=0, has_side_effects=True),
        name="tree_solve",
    )(
        right_sides,
        lower_inverse,
        upper_inverse,
        lower_blocks,
        upper_blocks,
        node_widths,
        far_levels,
        owner_level,
    )


def solution(mesh):
    spans = tuple(mesh.shape[axis] for axis in AXES)
    split = P(AXES)
    return jax.shard_map(
        functools.partial(local, spans),
        mesh=mesh,
        in_specs=(split,) * 7 + (P(),),
        out_specs=split,
        check_vma=False,
    )
```

profile of v0, /device:TPU:0, one launch (start us, length us, event | category | flops | bytes accessed | tf_op | source)
XLA Modules:
  0.0 50.0 jit_solution(17770108806762481978)
XLA Ops:
  0.0 48.5 %tree_solve.1 = f32[1,4,16,256]{3,2,1,0:T(8,128)} custom-call(f32[1,4,16,256]{3,2,1,0:T(8,128)} %rights_hbm.1, bf16[1,4,256,256]{3,2,1,0:T(8,128)(2,1)} %lower_inverse_hbm.1, bf16[1,4,256,256]{3,2,1,0:T(8,128)(2,1)} %upper_inverse_hbm.1, bf16[1,4,2,256,256]{4,3,2,1,0:T(8,128)(2,1)} %lower_blocks_hbm.1, bf16[1,4,2,256,256]{4,3,2,1,0:T(8,128)(2,1)} %upper_blocks_hbm.1, ...), custom_call_target="tpu_custom_call" | custom-call | tf_op jit(solution)/shard_map/tree_solve/pallas_call | solution.py:406
  48.5 1.5 %copy.10 = f32[1,4,16,256]{3,2,1,0:T(8,128)} copy(f32[1,4,16,256]{3,2,1,0:T(8,128)} %tree_solve.1) | data formatting | bytes 131072
where the time goes:
time: 50.2 us; the launch traced here: 50 us
  Pallas kernels  48.5 us (97%)
  local copies, waits for them, and re-layouts  1.47 us (3%)
    pallas_call x1, Pallas kernels, local(): pl.pallas_call(functools.partial(kernel, spans, plans, down_plans), out_s...  48.5 us
    unnamed x1, local copies, waits for them, and re-layouts  1.47 us

commit v1 on v0

--- a/solution.py
+++ b/solution.py
@@ -47,12 +47,14 @@
 
 HANDOUT = {
     2: ((1, False, 0),),
-    3: ((2, False, 0),(1, False, 1)),
-    4: ((2, False, 1),(1, True, 0)),
+    3: ((2, False, 0), (1, False, 1)),
+    4: ((2, False, 1), (1, True, 0)),
     5: ((1, True, 1),),
 }
 NEAR_BITS = 2
 NEAR = 2**NEAR_BITS
+CHAIN, TOP_SOLVE, SUB_SOLVE, BACK = range(4)
+SOURCES = {CHAIN: 0, TOP_SOLVE: 1, SUB_SOLVE: 1, BACK: 2}
 
 
 def kernel(
@@ -79,14 +81,22 @@
     replicas,
     fars,
     bases,
+    scattered,
+    doubled,
+    whole,
     load_sems,
     send_sems,
     recv_sems,
     bulk_send_sems,
     bulk_recv_sems,
+    spread_send_sems,
+    spread_recv_sems,
 ):
     layer_span, row_span, col_span = spans
+    col_bits = col_span.bit_length() - 1
+    layer_size = row_span * col_span
     upper_levels = len(plans)
+    top, sub = upper_levels, upper_levels - 1
     layer_at = lax.axis_index("gz")
     row_at = lax.axis_index("row")
     col_at = lax.axis_index("col")
@@ -94,7 +104,7 @@
 
     def peer(offset):
         return (
-            flip_bits(layer_at, offset // (row_span * col_span)),
+            flip_bits(layer_at, offset // layer_size),
             flip_bits(row_at, offset // col_span % row_span),
             flip_bits(col_at, offset % col_span),
         )
@@ -132,25 +142,39 @@
     my_level = spread(owner_ref[device])
     zeros = jnp.zeros((RHS, W), jnp.float32)
 
+    steps = []
+    for bit in range(upper_levels):
+        size = 1 << bit
+        steps.append(size - 2 * size * lax.rem(lax.div(device, size), 2))
+
+    def level_at(offset):
+        at = device
+        for bit in range(upper_levels):
+            if offset >> bit & 1:
+                at = at + steps[bit]
+        return owner_ref[at]
+
     def padded(slot, values):
         return jnp.where(inside[slot], values, 0.0)
 
-    counts = [0, 0]
+    counts = [0, 0, 0]
     sends = []
 
     def launch(rounded, phase):
-        outbox = counts[0]
-        counts[0] += 1
-        outgoing[outbox] = rounded
+        outbox, amount = counts[0], len(rounded)
+        counts[0] += amount
+        for index, part in enumerate(rounded):
+            outgoing[outbox + index] = part
         copies = []
         for offset in phase:
-            at = counts[1]
-            counts[1] += 1
+            at, message = counts[1], counts[2]
+            counts[1] += amount
+            counts[2] += 1
             copy = pltpu.make_async_remote_copy(
-                src_ref=outgoing.at[outbox],
-                dst_ref=incoming.at[at],
-                send_sem=send_sems.at[at],
-                recv_sem=recv_sems.at[at],
+                src_ref=outgoing.at[pl.ds(outbox, amount)],
+                dst_ref=incoming.at[pl.ds(at, amount)],
+                send_sem=send_sems.at[message],
+                recv_sem=recv_sems.at[message],
                 device_id=peer(offset),
                 device_id_type=pl.DeviceIdType.MESH,
             )
@@ -180,18 +204,102 @@
             received.add(name)
             bulk[name].wait_recv()
 
-    def exchange(values, plan, narrow, beside):
+    def exchange(values, plan, narrow, besides):
         for index, phase in enumerate(plan):
-            rounded = half(values)
+            rounded = [half(value) for value in values]
             copies = launch(rounded, phase)
-            if index == 0:
-                beside()
+            if index < len(besides):
+                besides[index]()
             if narrow:
-                values = rounded.astype(jnp.float32)
+                values = [part.astype(jnp.float32) for part in rounded]
             for copy, at in copies:
                 copy.wait_recv()
-                values = values + incoming[at].astype(jnp.float32)
+                values = [
+                    value + incoming[at + part].astype(jnp.float32)
+                    for part, value in enumerate(values)
+                ]
         return values
+
+    strip = W // row_span
+    my_strip = pl.ds(pl.multiple_of(row_at * strip, strip), strip)
+    stream_level = {CHAIN: sub, TOP_SOLVE: top, SUB_SOLVE: sub, BACK: sub}
+    spreads = []
+    spread_waits = {}
+
+    def spread_copy(key, source, target, offset):
+        at = len(spreads)
+        copy = pltpu.make_async_remote_copy(
+            src_ref=source,
+            dst_ref=target,
+            send_sem=spread_send_sems.at[at],
+            recv_sem=spread_recv_sems.at[at],
+            device_id=peer(offset),
+            device_id_type=pl.DeviceIdType.MESH,
+        )
+        copy.start()
+        spreads.append(copy)
+        spread_waits.setdefault(key, []).append(copy)
+
+    def await_spread(key):
+        for copy in spread_waits.pop(key, ()):
+            copy.wait_recv()
+
+    held = {}
+    for level in (sub, top):
+        plane = []
+        place = jnp.int32(0)
+        for step in range(row_span):
+            found = [
+                level_at(step * col_span + offset) == level for offset in range(col_span)
+            ]
+            place = jnp.where(found[0], step, place)
+            plane.append(found)
+        known_here = []
+        for bit in range(col_bits + 1):
+            here = jnp.int32(1)
+            for found in plane:
+                for offset in range(1 << bit):
+                    here = jnp.where(found[offset], 0, here)
+            known_here.append(here)
+        held[level] = (place, known_here)
+
+    def scatter_rows(source, matrix):
+        for step in range(1, row_span):
+            start = pl.multiple_of(flip_bits(row_at, step) * strip, strip)
+            spread_copy(
+                ("scatter", source),
+                matrix.at[pl.ds(start, strip)],
+                scattered[source].at[step],
+                step * col_span,
+            )
+        scattered[source][0] = matrix[my_strip]
+
+    def merged(stream, stage):
+        place, known_here = held[stream_level[stream]]
+        if stage == 0:
+            await_spread(("scatter", SOURCES[stream]))
+            return scattered[SOURCES[stream]][place]
+        await_spread(("double", stream, stage - 1))
+        return doubled[stream][stage - 1][known_here[stage - 1]]
+
+    def double_cols(stream, stage):
+        doubled[stream][stage][0] = merged(stream, stage)
+        spread_copy(
+            ("double", stream, stage),
+            doubled[stream][stage].at[0],
+            doubled[stream][stage].at[1],
+            1 << stage if stage < col_bits else layer_size,
+        )
+
+    def gather_rows(stream, stage):
+        whole[stream][my_strip] = merged(stream, stage)
+        for step in range(1, row_span):
+            spread_copy(
+                ("gather", stream),
+                whole[stream].at[my_strip],
+                whole[stream].at[my_strip],
+                step * col_span,
+            )
 
     pending = [None] + [zeros for _ in range(upper_levels)]
 
@@ -217,18 +325,29 @@
     forward[2] = padded(2, times(half(rights[2] - near), lower_inverse[2]))
     pending[1] = pending[1] + times(half(forward[2]), lower_blocks[2, 0])
     scatter_up(times(half(forward[2]), lower_blocks[2, 1]), 2, 1)
+    for level in (sub, top):
+        pending[level] = pending[level] - jnp.where(my_level == level, rights[OWN], 0.0)
 
     pl.semaphore_wait(barrier, len(partners))
 
     wide_columns = lax.broadcasted_iota(jnp.int32, (W, W), 1)
+    wide_rows = lax.broadcasted_iota(jnp.int32, (W, W), 0)
+
+    def own_columns(matrix):
+        kept = jnp.where(
+            wide_columns < widths_ref[0, OWN], matrix.astype(jnp.float32), 0.0
+        )
+        return half(kept)
+
+    def own_rows(matrix):
+        return jnp.where(wide_rows < widths_ref[0, OWN], matrix, 0.0)
 
     def lower_product(block_id):
-        kept = jnp.where(
-            wide_columns < widths_ref[0, OWN],
-            lower_blocks[OWN, block_id].astype(jnp.float32),
-            0.0,
-        )
-        return jnp.dot(half(kept), lower_inverse[OWN], preferred_element_type=jnp.float32)
+        return jnp.dot(
+            own_columns(lower_blocks[OWN, block_id]),
+            lower_inverse[OWN],
+            preferred_element_type=jnp.float32,
+        )
 
     def upper_product(slot, block_id):
         return jnp.dot(
@@ -242,12 +361,12 @@
 
     far_is_near = jnp.full((W, W), far_ref[0, OWN], jnp.int32) == 1
 
-    own_forward = [zeros]
+    own_base = [zeros]
     residue = [None]
 
     def own_solve(level):
-        solved = padded(OWN, times(residue[0], lower_inverse[OWN]))
-        own_forward[0] = own_forward[0] + jnp.where(my_level == level, solved, 0.0)
+        solved = times(residue[0], fused[2])
+        own_base[0] = own_base[0] + jnp.where(my_level == level, solved, 0.0)
 
     def far_up(level):
         product = jnp.where(my_level == level, times(residue[0], fused[1]), 0.0)
@@ -256,34 +375,8 @@
                 far[OWN] == target - level, product, 0.0
             )
 
-    wide_rows = lax.broadcasted_iota(jnp.int32, (W, W), 0)
-
-    def upper_kept(block_id):
-        return jnp.where(
-            wide_rows < widths_ref[0, OWN], upper_product(OWN, block_id), 0.0
-        )
-
-    def beside_up(level):
-        if level == 1:
-            fars[0] = far[OWN].astype(jnp.float32)
-            for offset in range(1, NEAR):
-                hand_out(("far", offset), fars.at[0], fars.at[offset], offset)
-            far_product = lower_product(1)
-            fused[1] = half(far_product)
-            fused[0] = half(lower_product(0) + jnp.where(far_is_near, far_product, 0.0))
-            loads[5].wait()
-            loads[6].wait()
-            far_product = upper_kept(1)
-            replicas[0, 1] = half(far_product)
-            replicas[0, 0] = half(upper_kept(0) + jnp.where(far_is_near, far_product, 0.0))
-        else:
-            far_up(level - 1)
-            own_solve(level - 1)
-        if level == upper_levels:
-            bases[0] = padded(OWN, split_times(own_forward[0], upper_inverse[OWN]))
-            for offset in reversed(range(1, NEAR)):
-                hand_out(("base", offset), bases.at[0], bases.at[offset], offset)
-        for offset, relayed, block_id in HANDOUT.get(level, ()):
+    def hand_out_row(slot_of):
+        for offset, relayed, block_id in HANDOUT.get(slot_of, ()):
             kept = 2 if relayed else 0
             if relayed:
                 await_bulk((2, False, block_id))
@@ -293,20 +386,101 @@
                 replicas.at[kept + offset, block_id],
                 offset,
             )
-        if 3 <= level < 3 + LOCAL_COUNT:
-            slot = level - 3
-            for block_id in range(NB):
-                fused[4 + 2 * slot + block_id] = half(upper_product(slot, block_id))
-
-    for level in range(1, upper_levels + 1):
+
+    def leaf_products(slot):
+        for block_id in range(NB):
+            fused[3 + 2 * slot + block_id] = half(upper_product(slot, block_id))
+
+    leaf_base = [None] * LOCAL_COUNT
+
+    def beside_up(level):
+        if level == 1:
+            fars[0] = far[OWN][: fars.shape[1], : fars.shape[2]].astype(jnp.float32)
+            for offset in range(1, NEAR):
+                hand_out(("far", offset), fars.at[0], fars.at[offset], offset)
+            far_product = lower_product(1)
+            fused[0] = half(lower_product(0) + jnp.where(far_is_near, far_product, 0.0))
+            scatter_rows(0, fused.at[0])
+            fused[1] = half(far_product)
+            loads[5].wait()
+            loads[6].wait()
+            fused[2] = half(
+                own_rows(
+                    jnp.dot(
+                        own_columns(upper_inverse[OWN]),
+                        lower_inverse[OWN],
+                        preferred_element_type=jnp.float32,
+                    )
+                )
+            )
+            scatter_rows(1, fused.at[2])
+            far_product = own_rows(upper_product(OWN, 1))
+            replicas[0, 1] = half(far_product)
+            replicas[0, 0] = half(
+                own_rows(upper_product(OWN, 0)) + jnp.where(far_is_near, far_product, 0.0)
+            )
+            scatter_rows(2, replicas.at[0, 0])
+            return
+        if level < sub:
+            far_up(level - 1)
+        own_solve(level - 1)
+        if level < sub:
+            for stream in (CHAIN, TOP_SOLVE, SUB_SOLVE):
+                double_cols(stream, level - 2)
+            if level > 2:
+                double_cols(BACK, level - 3)
+        hand_out_row(level)
+        if level - 2 < LOCAL_COUNT:
+            leaf_products(level - 2)
+
+    def beside_sub(index):
+        if index == 0:
+            bases[0] = own_base[0]
+            for offset in reversed(range(1, NEAR)):
+                hand_out(("base", offset), bases.at[0], bases.at[offset], offset)
+            double_cols(TOP_SOLVE, col_bits)
+            gather_rows(CHAIN, col_bits)
+            gather_rows(SUB_SOLVE, col_bits)
+            double_cols(BACK, col_bits - 1)
+        if index == len(plans[sub - 1]) - 1:
+            gather_rows(TOP_SOLVE, col_bits + 1)
+            gather_rows(BACK, col_bits)
+            hand_out_row(sub + 1)
+
+    for level in range(1, sub):
         gathered = exchange(
-            pending[level], plans[level - 1], False, functools.partial(beside_up, level)
-        )
+            [pending[level]], plans[level - 1], False, [functools.partial(beside_up, level)]
+        )[0]
         residue[0] = half(rights[OWN] - gathered)
-        if level < upper_levels:
-            product = times(residue[0], fused[0])
-            pending[level + 1] = pending[level + 1] + jnp.where(my_level == level, product, 0.0)
-    own_solve(upper_levels)
+        product = times(residue[0], fused[0])
+        pending[level + 1] = pending[level + 1] + jnp.where(my_level == level, product, 0.0)
+    far_up(sub - 1)
+
+    def first_beside():
+        beside_up(sub)
+        beside_sub(0)
+
+    sums = exchange(
+        [pending[sub], pending[top]],
+        plans[sub - 1],
+        False,
+        [first_beside]
+        + [functools.partial(beside_sub, index) for index in range(1, len(plans[sub - 1]))],
+    )
+    sub_residue = half(-sums[0])
+    await_spread(("gather", CHAIN))
+    layer_sum = sums[1] + times(sub_residue, whole[CHAIN][...])
+    sub_base = [None]
+
+    def beside_top():
+        await_spread(("gather", SUB_SOLVE))
+        sub_base[0] = times(sub_residue, whole[SUB_SOLVE][...])
+        for slot in range(LOCAL_COUNT):
+            leaf_base[slot] = split_times(forward[slot], upper_inverse[slot])
+        await_spread(("gather", TOP_SOLVE))
+        await_spread(("gather", BACK))
+
+    total = exchange([layer_sum], plans[top - 1], False, [beside_top])[0]
 
     known = [None] * (upper_levels + 1)
 
@@ -316,10 +490,8 @@
             chosen = chosen + jnp.where(far[slot] == level - below, known[level], 0.0)
         return half(chosen)
 
-    own_solution = zeros
-    leaf_base = [None] * LOCAL_COUNT
     far_part = [zeros]
-    near_levels = [owner_ref[flip_bits(device, offset)] for offset in range(NEAR)]
+    near_levels = [level_at(offset) for offset in range(NEAR)]
 
     def holder(level):
         offset_of = jnp.int32(0)
@@ -334,51 +506,51 @@
             return
         at, _ = holder(level)
         reach = fars[at]
+        reach = jnp.concatenate([reach] * (W // reach.shape[1]), axis=1)
+        reach = jnp.concatenate([reach] * (RHS // reach.shape[0]), axis=0)
         chosen = zeros
         for target in range(level + 2, upper_levels + 1):
             chosen = chosen + jnp.where(reach == float(target - level), known[target], 0.0)
         far_part[0] = times(half(chosen), replicas[at, 1])
 
-    def beside_down(level):
-        if level == upper_levels:
-            for slot in range(LOCAL_COUNT):
-                leaf_base[slot] = split_times(forward[slot], upper_inverse[slot])
-        else:
-            prepare(level - 1)
-
-    for level in range(upper_levels, 0, -1):
-        if level == upper_levels:
-            solved = padded(OWN, split_times(own_forward[0], upper_inverse[OWN]))
-            solved = jnp.where(my_level == level, solved, 0.0)
-        else:
-            at, found = holder(level)
-            solved = bases[at] - far_part[0] - times(half(known[level + 1]), replicas[at, 0])
-            solved = jnp.where(spread(found) == 1, solved, 0.0)
+    solved = times(half(-total), whole[TOP_SOLVE][...])
+    own_solution = jnp.where(my_level == top, solved, 0.0)
+    known[top] = half(solved).astype(jnp.float32)
+    solved = sub_base[0] - times(half(solved), whole[BACK][...])
+    own_solution = own_solution + jnp.where(my_level == sub, solved, 0.0)
+    known[sub] = half(solved).astype(jnp.float32)
+    for name in bulk:
+        await_bulk(name)
+    prepare(sub - 1)
+
+    for level in range(sub - 1, 0, -1):
+        at, found = holder(level)
+        solved = bases[at] - far_part[0] - times(half(known[level + 1]), replicas[at, 0])
+        solved = jnp.where(spread(found) == 1, solved, 0.0)
         own_solution = own_solution + jnp.where(my_level == level, solved, 0.0)
         if down_plans[level - 1]:
             known[level] = exchange(
-                solved, down_plans[level - 1], True, functools.partial(beside_down, level)
-            )
+                [solved], down_plans[level - 1], True, [functools.partial(prepare, level - 1)]
+            )[0]
         else:
             known[level] = half(solved).astype(jnp.float32)
-            beside_down(level)
-        if level == upper_levels:
-            for name in bulk:
-                await_bulk(name)
-    leaf_base[2] = leaf_base[2] - times(pick(2, 0, 2), fused[4 + 2 * 2 + 1])
+            prepare(level - 1)
+    leaf_base[2] = leaf_base[2] - times(pick(2, 0, 2), fused[3 + 2 * 2 + 1])
     out_ref[0, OWN] = own_solution
 
     nearest = half(known[1])
-    root = padded(2, leaf_base[2] - times(nearest, fused[4 + 2 * 2]))
+    root = padded(2, leaf_base[2] - times(nearest, fused[3 + 2 * 2]))
     out_ref[0, 2] = root
     for slot in range(2):
-        solved = leaf_base[slot] - times(pick(slot, -1, 1), fused[4 + 2 * slot + 1])
-        solved = solved - times(half(root), fused[4 + 2 * slot])
+        solved = leaf_base[slot] - times(pick(slot, -1, 1), fused[3 + 2 * slot + 1])
+        solved = solved - times(half(root), fused[3 + 2 * slot])
         out_ref[0, slot] = padded(slot, solved)
 
     for copy, _ in sends:
         copy.wait_send()
     for copy in bulk.values():
+        copy.wait_send()
+    for copy in spreads:
         copy.wait_send()
 
 
@@ -395,12 +567,21 @@
 ):
     layer_span, row_span, col_span = spans
     upper_levels = (layer_span * row_span * col_span).bit_length() - 1
-    plans = [exchange_plan(level) for level in range(1, upper_levels + 1)]
-    down_plans = [exchange_plan(level, NEAR_BITS) for level in range(1, upper_levels)]
-    down_plans.append(plans[-1])
-    phases = sum(len(plan) for plan in plans + down_plans)
-    messages = sum(len(phase) for plan in plans + down_plans for phase in plan)
+    row_bits, col_bits = row_span.bit_length() - 1, col_span.bit_length() - 1
+    top, sub = upper_levels, upper_levels - 1
+    plans = [exchange_plan(level) for level in range(1, sub)]
+    plans.append(exchange_plan(col_bits) + exchange_plan(sub, col_bits))
+    plans.append(exchange_plan(top, sub))
+    down_plans = [exchange_plan(level, NEAR_BITS) for level in range(1, sub)]
+    vectors = [1] * (sub - 1) + [2, 1] + [1] * len(down_plans)
+    routes = list(zip(vectors, plans + down_plans))
+    phases = sum(amount * len(plan) for amount, plan in routes)
+    messages = sum(len(phase) for _, plan in routes for phase in plan)
+    boxes = sum(amount * len(phase) for amount, plan in routes for phase in plan)
     handed = 2 * (NEAR - 1) + sum(len(row) for row in HANDOUT.values())
+    streams, sources = len(SOURCES), len(set(SOURCES.values()))
+    strip = W // row_span
+    spread_count = (sources + streams) * (row_span - 1) + streams * col_bits + 1
     hbm = pl.BlockSpec(memory_space=pl.ANY)
     smem = pl.BlockSpec(memory_space=pltpu.SMEM)
     return pl.pallas_call(
@@ -415,16 +596,21 @@
             pltpu.VMEM(lower_blocks.shape[1:], jnp.bfloat16),
             pltpu.VMEM(upper_blocks.shape[1:], jnp.bfloat16),
             pltpu.VMEM((phases, RHS, W), jnp.bfloat16),
-            pltpu.VMEM((messages, RHS, W), jnp.bfloat16),
-            pltpu.VMEM((4 + NB * LOCAL_COUNT, W, W), jnp.bfloat16),
+            pltpu.VMEM((boxes, RHS, W), jnp.bfloat16),
+            pltpu.VMEM((3 + NB * LOCAL_COUNT, W, W), jnp.bfloat16),
             pltpu.VMEM((NEAR, NB, W, W), jnp.bfloat16),
+            pltpu.VMEM((NEAR, 8, 128), jnp.float32),
             pltpu.VMEM((NEAR, RHS, W), jnp.float32),
-            pltpu.VMEM((NEAR, RHS, W), jnp.float32),
+            [pltpu.VMEM((row_span, strip, W), jnp.bfloat16)] * sources,
+            [[pltpu.VMEM((2, strip, W), jnp.bfloat16)] * (col_bits + 1)] * streams,
+            [pltpu.VMEM((W, W), jnp.bfloat16)] * streams,
             pltpu.SemaphoreType.DMA((7,)),
             pltpu.SemaphoreType.DMA((messages,)),
             pltpu.SemaphoreType.DMA((messages,)),
             pltpu.SemaphoreType.DMA((handed,)),
             pltpu.SemaphoreType.DMA((handed,)),
+            pltpu.SemaphoreType.DMA((spread_count,)),
+            pltpu.SemaphoreType.DMA((spread_count,)),
         ],
         compiler_params=pltpu.CompilerParams(collective_id=0, has_side_effects=True),
         name="tree_solve",

time: 50.2 us -> 47.5 us (0.946)
  Pallas kernels: 48.5 us -> 45.8 us
    pallas_call x1, Pallas kernels: 48.5 us -> 45.8 us  [local(): pl.pallas_call(functools.partial(kernel, spans, plans, down_plans), out_s...]
where the time goes in v1:
time: 47.5 us; the launch traced here: 47.3 us
  Pallas kernels  45.8 us (96%)
  local copies, waits for them, and re-layouts  1.47 us (3%)
    pallas_call x1, Pallas kernels, local(): pl.pallas_call(functools.partial(kernel, spans, plans, down_plans), out_s...  45.8 us
    unnamed x1, local copies, waits for them, and re-layouts  1.47 us

profile of v1, /device:TPU:0, one launch (start us, length us, event | category | flops | bytes accessed | tf_op | source)
XLA Modules:
  0.0 47.3 jit_solution(11711298247870864689)
XLA Ops:
  0.0 45.8 %tree_solve.1 = f32[1,4,16,256]{3,2,1,0:T(8,128)} custom-call(f32[1,4,16,256]{3,2,1,0:T(8,128)} %rights_hbm.1, bf16[1,4,256,256]{3,2,1,0:T(8,128)(2,1)} %lower_inverse_hbm.1, bf16[1,4,256,256]{3,2,1,0:T(8,128)(2,1)} %upper_inverse_hbm.1, bf16[1,4,2,256,256]{4,3,2,1,0:T(8,128)(2,1)} %lower_blocks_hbm.1, bf16[1,4,2,256,256]{4,3,2,1,0:T(8,128)(2,1)} %upper_blocks_hbm.1, ...), custom_call_target="tpu_custom_call" | custom-call | tf_op jit(solution)/shard_map/tree_solve/pallas_call | solution.py:587
  45.8 1.5 %copy.10 = f32[1,4,16,256]{3,2,1,0:T(8,128)} copy(f32[1,4,16,256]{3,2,1,0:T(8,128)} %tree_solve.1) | data formatting | bytes 131072

commit v2 on v1

--- a/solution.py
+++ b/solution.py
@@ -26,12 +26,13 @@
     return flipped
 
 
-def exchange_plan(level, low=0):
+def exchange_plan(bits):
     phases = []
-    while low < level:
-        high = min(low + 4, level)
-        phases.append([step << low for step in range((1 << (high - low)) - 1, 0, -1)])
-        low = high
+    for low in range(0, len(bits), 4):
+        offsets = [0]
+        for bit in bits[low : low + 4]:
+            offsets += [offset + (1 << bit) for offset in offsets]
+        phases.append(offsets[:0:-1])
     return phases
 
 
@@ -45,12 +46,6 @@
     return values.astype(jnp.bfloat16)
 
 
-HANDOUT = {
-    2: ((1, False, 0),),
-    3: ((2, False, 0), (1, False, 1)),
-    4: ((2, False, 1), (1, True, 0)),
-    5: ((1, True, 1),),
-}
 NEAR_BITS = 2
 NEAR = 2**NEAR_BITS
 CHAIN, TOP_SOLVE, SUB_SOLVE, BACK = range(4)
@@ -78,7 +73,11 @@
     outgoing,
     incoming,
     fused,
-    replicas,
+    near_blocks,
+    far_blocks,
+    second,
+    beside_near,
+    beside_far,
     fars,
     bases,
     scattered,
@@ -126,7 +125,8 @@
         load.start()
 
     barrier = pltpu.get_barrier_semaphore()
-    partners = sorted({offset for plan in plans for phase in plan for offset in phase})
+    partners = {offset for plan in plans for phase in plan for offset in phase}
+    partners = sorted(partners | {step * col_span for step in range(1, row_span)})
     for offset in partners:
         pl.semaphore_signal(
             barrier, inc=1, device_id=peer(offset), device_id_type=pl.DeviceIdType.MESH
@@ -139,7 +139,8 @@
 
     inside = [columns < widths_ref[0, slot] for slot in range(LOCAL_COUNT + 1)]
     far = [spread(far_ref[0, slot]) for slot in range(LOCAL_COUNT + 1)]
-    my_level = spread(owner_ref[device])
+    my_level_scalar = owner_ref[device]
+    my_level = spread(my_level_scalar)
     zeros = jnp.zeros((RHS, W), jnp.float32)
 
     steps = []
@@ -325,7 +326,7 @@
     forward[2] = padded(2, times(half(rights[2] - near), lower_inverse[2]))
     pending[1] = pending[1] + times(half(forward[2]), lower_blocks[2, 0])
     scatter_up(times(half(forward[2]), lower_blocks[2, 1]), 2, 1)
-    for level in (sub, top):
+    for level in range(1, upper_levels + 1):
         pending[level] = pending[level] - jnp.where(my_level == level, rights[OWN], 0.0)
 
     pl.semaphore_wait(barrier, len(partners))
@@ -375,33 +376,22 @@
                 far[OWN] == target - level, product, 0.0
             )
 
-    def hand_out_row(slot_of):
-        for offset, relayed, block_id in HANDOUT.get(slot_of, ()):
-            kept = 2 if relayed else 0
-            if relayed:
-                await_bulk((2, False, block_id))
-            hand_out(
-                (offset, relayed, block_id),
-                replicas.at[kept, block_id],
-                replicas.at[kept + offset, block_id],
-                offset,
-            )
-
     def leaf_products(slot):
         for block_id in range(NB):
             fused[3 + 2 * slot + block_id] = half(upper_product(slot, block_id))
 
     leaf_base = [None] * LOCAL_COUNT
 
+    halves = {}
+
     def beside_up(level):
         if level == 1:
-            fars[0] = far[OWN][: fars.shape[1], : fars.shape[2]].astype(jnp.float32)
-            for offset in range(1, NEAR):
-                hand_out(("far", offset), fars.at[0], fars.at[offset], offset)
             far_product = lower_product(1)
             fused[0] = half(lower_product(0) + jnp.where(far_is_near, far_product, 0.0))
+            beside_near[0] = fused[0]
             scatter_rows(0, fused.at[0])
             fused[1] = half(far_product)
+            beside_far[0] = fused[1]
             loads[5].wait()
             loads[6].wait()
             fused[2] = half(
@@ -414,59 +404,82 @@
                 )
             )
             scatter_rows(1, fused.at[2])
+            hand_out("beside near", fused.at[0], beside_near.at[1], col_span)
             far_product = own_rows(upper_product(OWN, 1))
-            replicas[0, 1] = half(far_product)
-            replicas[0, 0] = half(
+            far_blocks[0] = half(far_product)
+            near_blocks[0] = half(
                 own_rows(upper_product(OWN, 0)) + jnp.where(far_is_near, far_product, 0.0)
             )
-            scatter_rows(2, replicas.at[0, 0])
+            fars[0] = far[OWN][: fars.shape[1], : fars.shape[2]].astype(jnp.float32)
             return
-        if level < sub:
-            far_up(level - 1)
-        own_solve(level - 1)
         if level < sub:
             for stream in (CHAIN, TOP_SOLVE, SUB_SOLVE):
                 double_cols(stream, level - 2)
+            if level == 2:
+                scatter_rows(2, near_blocks.at[0])
             if level > 2:
                 double_cols(BACK, level - 3)
-        hand_out_row(level)
-        if level - 2 < LOCAL_COUNT:
-            leaf_products(level - 2)
-
-    def beside_sub(index):
-        if index == 0:
-            bases[0] = own_base[0]
-            for offset in reversed(range(1, NEAR)):
-                hand_out(("base", offset), bases.at[0], bases.at[offset], offset)
+        if level == sub - 1:
+            hand_out("beside far", fused.at[1], beside_far.at[1], col_span)
+            hand_out("near", near_blocks.at[0], near_blocks.at[1], 1)
+        own_solve(level - 1)
+        if level == sub:
             double_cols(TOP_SOLVE, col_bits)
             gather_rows(CHAIN, col_bits)
             gather_rows(SUB_SOLVE, col_bits)
             double_cols(BACK, col_bits - 1)
-        if index == len(plans[sub - 1]) - 1:
-            gather_rows(TOP_SOLVE, col_bits + 1)
-            gather_rows(BACK, col_bits)
-            hand_out_row(sub + 1)
+            await_bulk("near")
+            second[0] = near_blocks[pair_place]
+            hand_out("second", second.at[0], second.at[1], 2)
+            hand_out("far", far_blocks.at[0], far_blocks.at[1], 1)
+            hand_out("fars", fars.at[0], fars.at[1], 1)
+        if level - 2 < LOCAL_COUNT:
+            leaf_products(level - 2)
+
+    near_levels = [level_at(offset) for offset in range(NEAR)]
+    pair_place = jnp.where(near_levels[1] == 2, 1, 0)
+    second_place = jnp.where(near_levels[2] == 2, 1, jnp.where(near_levels[3] == 2, 1, 0))
+
+    def holder(level):
+        offset_of = jnp.int32(0)
+        for offset in range(2**level):
+            offset_of = jnp.where(near_levels[offset] == level, offset, offset_of)
+        return offset_of
 
     for level in range(1, sub):
+        if level == sub - 1:
+            for copy, at in launch([half(pending[sub]), half(pending[top])], [col_span]):
+                halves["copy"], halves["at"] = copy, at
         gathered = exchange(
             [pending[level]], plans[level - 1], False, [functools.partial(beside_up, level)]
         )[0]
-        residue[0] = half(rights[OWN] - gathered)
-        product = times(residue[0], fused[0])
-        pending[level + 1] = pending[level + 1] + jnp.where(my_level == level, product, 0.0)
-    far_up(sub - 1)
-
-    def first_beside():
-        beside_up(sub)
-        beside_sub(0)
-
-    sums = exchange(
-        [pending[sub], pending[top]],
-        plans[sub - 1],
-        False,
-        [first_beside]
-        + [functools.partial(beside_sub, index) for index in range(1, len(plans[sub - 1]))],
-    )
+        residue[0] = half(-gathered)
+        if level < sub - 1:
+            product = times(residue[0], fused[0])
+            pending[level + 1] = pending[level + 1] + jnp.where(
+                my_level == level, product, 0.0
+            )
+            far_up(level)
+
+    across = level_at(col_span)
+    on_side = jnp.where(across == sub - 1, 1, 0)
+    here = spread(jnp.where(my_level_scalar == sub - 1, 1, on_side)) == 1
+    halves["copy"].wait_recv()
+    await_bulk("beside near")
+    await_bulk("beside far")
+    products = [
+        times(residue[0], beside_near[on_side]),
+        times(residue[0], beside_far[on_side]),
+    ]
+    values = [
+        pending[level]
+        + incoming[halves["at"] + index].astype(jnp.float32)
+        + jnp.where(here, products[index], 0.0)
+        for index, level in enumerate((sub, top))
+    ]
+    sums = exchange(values, plans[sub - 1], False, [functools.partial(beside_up, sub)])
+    gather_rows(TOP_SOLVE, col_bits + 1)
+    gather_rows(BACK, col_bits)
     sub_residue = half(-sums[0])
     await_spread(("gather", CHAIN))
     layer_sum = sums[1] + times(sub_residue, whole[CHAIN][...])
@@ -490,51 +503,48 @@
             chosen = chosen + jnp.where(far[slot] == level - below, known[level], 0.0)
         return half(chosen)
 
-    far_part = [zeros]
-    near_levels = [level_at(offset) for offset in range(NEAR)]
-
-    def holder(level):
-        offset_of = jnp.int32(0)
-        found = jnp.int32(0)
-        for offset in range(min(NEAR, 2**level)):
-            offset_of = jnp.where(near_levels[offset] == level, offset, offset_of)
-            found = jnp.where(near_levels[offset] == level, 1, found)
-        return offset_of, found
-
-    def prepare(level):
-        if level < 1 or level + 2 > upper_levels:
-            return
-        at, _ = holder(level)
-        reach = fars[at]
-        reach = jnp.concatenate([reach] * (W // reach.shape[1]), axis=1)
-        reach = jnp.concatenate([reach] * (RHS // reach.shape[0]), axis=0)
-        chosen = zeros
-        for target in range(level + 2, upper_levels + 1):
-            chosen = chosen + jnp.where(reach == float(target - level), known[target], 0.0)
-        far_part[0] = times(half(chosen), replicas[at, 1])
-
     solved = times(half(-total), whole[TOP_SOLVE][...])
     own_solution = jnp.where(my_level == top, solved, 0.0)
     known[top] = half(solved).astype(jnp.float32)
     solved = sub_base[0] - times(half(solved), whole[BACK][...])
     own_solution = own_solution + jnp.where(my_level == sub, solved, 0.0)
     known[sub] = half(solved).astype(jnp.float32)
+
+    for level in range(sub - 1, NEAR_BITS, -1):
+        chosen = zeros
+        for target in range(level + 1, upper_levels + 1):
+            chosen = chosen + jnp.where(my_level + far[OWN] == target, known[target], 0.0)
+        base = own_base[0] - times(half(chosen), far_blocks[0])
+        solved = base - times(half(known[level + 1]), near_blocks[0])
+        solved = jnp.where(my_level == level, solved, 0.0)
+        own_solution = own_solution + solved
+
+        def beside_down():
+            if level == NEAR_BITS + 1:
+                bases[0] = half(jnp.where(my_level == 1, own_base[0], base))
+                for offset in range(1, NEAR):
+                    hand_out(("base", offset), bases.at[0], bases.at[offset], offset)
+
+        known[level] = exchange([solved], down_plans[level - 1], True, [beside_down])[0]
     for name in bulk:
         await_bulk(name)
-    prepare(sub - 1)
-
-    for level in range(sub - 1, 0, -1):
-        at, found = holder(level)
-        solved = bases[at] - far_part[0] - times(half(known[level + 1]), replicas[at, 0])
-        solved = jnp.where(spread(found) == 1, solved, 0.0)
-        own_solution = own_solution + jnp.where(my_level == level, solved, 0.0)
-        if down_plans[level - 1]:
-            known[level] = exchange(
-                [solved], down_plans[level - 1], True, [functools.partial(prepare, level - 1)]
-            )[0]
-        else:
-            known[level] = half(solved).astype(jnp.float32)
-            prepare(level - 1)
+
+    at = holder(1)
+    reach = fars[at]
+    reach = jnp.concatenate([reach] * (W // reach.shape[1]), axis=1)
+    reach = jnp.concatenate([reach] * (RHS // reach.shape[0]), axis=0)
+    chosen = zeros
+    for target in range(3, upper_levels + 1):
+        chosen = chosen + jnp.where(reach == float(target - 1), known[target], 0.0)
+    base = bases[at].astype(jnp.float32) - times(half(chosen), far_blocks[at])
+    solved = bases[holder(2)].astype(jnp.float32) - times(
+        half(known[3]), second[second_place]
+    )
+    own_solution = own_solution + jnp.where(my_level == 2, solved, 0.0)
+    known[2] = half(solved).astype(jnp.float32)
+    solved = base - times(half(solved), near_blocks[at])
+    own_solution = own_solution + jnp.where(my_level == 1, solved, 0.0)
+    known[1] = half(solved).astype(jnp.float32)
     leaf_base[2] = leaf_base[2] - times(pick(2, 0, 2), fused[3 + 2 * 2 + 1])
     out_ref[0, OWN] = own_solution
 
@@ -567,18 +577,19 @@
 ):
     layer_span, row_span, col_span = spans
     upper_levels = (layer_span * row_span * col_span).bit_length() - 1
-    row_bits, col_bits = row_span.bit_length() - 1, col_span.bit_length() - 1
+    col_bits = col_span.bit_length() - 1
     top, sub = upper_levels, upper_levels - 1
-    plans = [exchange_plan(level) for level in range(1, sub)]
-    plans.append(exchange_plan(col_bits) + exchange_plan(sub, col_bits))
-    plans.append(exchange_plan(top, sub))
-    down_plans = [exchange_plan(level, NEAR_BITS) for level in range(1, sub)]
-    vectors = [1] * (sub - 1) + [2, 1] + [1] * len(down_plans)
-    routes = list(zip(vectors, plans + down_plans))
+    plans = [exchange_plan(list(range(level))) for level in range(1, sub)]
+    plans.append(exchange_plan(list(range(col_bits)) + [sub - 1]))
+    plans.append(exchange_plan([sub]))
+    down_plans = [[]] * NEAR_BITS
+    down_plans += [exchange_plan(list(range(level))) for level in range(NEAR_BITS + 1, sub)]
+    vectors = [1] * (sub - 1) + [2, 1, 2] + [1] * len(down_plans)
+    routes = list(zip(vectors, plans + [[[col_span]]] + down_plans))
     phases = sum(amount * len(plan) for amount, plan in routes)
     messages = sum(len(phase) for _, plan in routes for phase in plan)
     boxes = sum(amount * len(phase) for amount, plan in routes for phase in plan)
-    handed = 2 * (NEAR - 1) + sum(len(row) for row in HANDOUT.values())
+    handed = 6 + NEAR - 1
     streams, sources = len(SOURCES), len(set(SOURCES.values()))
     strip = W // row_span
     spread_count = (sources + streams) * (row_span - 1) + streams * col_bits + 1
@@ -598,9 +609,13 @@
             pltpu.VMEM((phases, RHS, W), jnp.bfloat16),
             pltpu.VMEM((boxes, RHS, W), jnp.bfloat16),
             pltpu.VMEM((3 + NB * LOCAL_COUNT, W, W), jnp.bfloat16),
-            pltpu.VMEM((NEAR, NB, W, W), jnp.bfloat16),
-            pltpu.VMEM((NEAR, 8, 128), jnp.float32),
-            pltpu.VMEM((NEAR, RHS, W), jnp.float32),
+            pltpu.VMEM((2, W, W), jnp.bfloat16),
+            pltpu.VMEM((2, W, W), jnp.bfloat16),
+            pltpu.VMEM((2, W, W), jnp.bfloat16),
+            pltpu.VMEM((2, W, W), jnp.bfloat16),
+            pltpu.VMEM((2, W, W), jnp.bfloat16),
+            pltpu.VMEM((2, 8, 128), jnp.float32),
+            pltpu.VMEM((NEAR, RHS, W), jnp.bfloat16),
             [pltpu.VMEM((row_span, strip, W), jnp.bfloat16)] * sources,
             [[pltpu.VMEM((2, strip, W), jnp.bfloat16)] * (col_bits + 1)] * streams,
             [pltpu.VMEM((W, W), jnp.bfloat16)] * streams,

time: 47.5 us -> 41.9 us (0.88)
  Pallas kernels: 45.8 us -> 40.2 us
    pallas_call x1, Pallas kernels: 45.8 us -> 40.2 us  [local(): pl.pallas_call(functools.partial(kernel, spans, plans, down_plans), out_s...]
where the time goes in v2:
time: 41.9 us; the launch traced here: 41.7 us
  Pallas kernels  40.2 us (96%)
  local copies, waits for them, and re-layouts  1.47 us (4%)
    pallas_call x1, Pallas kernels, local(): pl.pallas_call(functools.partial(kernel, spans, plans, down_plans), out_s...  40.2 us
    unnamed x1, local copies, waits for them, and re-layouts  1.47 us

profile of v2, /device:TPU:0, one launch (start us, length us, event | category | flops | bytes accessed | tf_op | source)
XLA Modules:
  0.0 41.7 jit_solution(14514841796422177482)
XLA Ops:
  0.0 40.2 %tree_solve.1 = f32[1,4,16,256]{3,2,1,0:T(8,128)} custom-call(f32[1,4,16,256]{3,2,1,0:T(8,128)} %rights_hbm.1, bf16[1,4,256,256]{3,2,1,0:T(8,128)(2,1)} %lower_inverse_hbm.1, bf16[1,4,256,256]{3,2,1,0:T(8,128)(2,1)} %upper_inverse_hbm.1, bf16[1,4,2,256,256]{4,3,2,1,0:T(8,128)(2,1)} %lower_blocks_hbm.1, bf16[1,4,2,256,256]{4,3,2,1,0:T(8,128)(2,1)} %upper_blocks_hbm.1, ...), custom_call_target="tpu_custom_call" | custom-call | tf_op jit(solution)/shard_map/tree_solve/pallas_call | solution.py:598
  40.2 1.5 %copy.10 = f32[1,4,16,256]{3,2,1,0:T(8,128)} copy(f32[1,4,16,256]{3,2,1,0:T(8,128)} %tree_solve.1) | data formatting | bytes 131072

commit v3 on v2

--- a/solution.py
+++ b/solution.py
@@ -77,7 +77,7 @@
     far_blocks,
     second,
     beside_near,
-    beside_far,
+    ahead,
     fars,
     bases,
     scattered,
@@ -125,7 +125,7 @@
         load.start()
 
     barrier = pltpu.get_barrier_semaphore()
-    partners = {offset for plan in plans for phase in plan for offset in phase}
+    partners = {offset for plan in plans + down_plans for phase in plan for offset in phase}
     partners = sorted(partners | {step * col_span for step in range(1, row_span)})
     for offset in partners:
         pl.semaphore_signal(
@@ -205,10 +205,10 @@
             received.add(name)
             bulk[name].wait_recv()
 
-    def exchange(values, plan, narrow, besides):
+    def exchange(values, plan, narrow, besides, started=None):
         for index, phase in enumerate(plan):
             rounded = [half(value) for value in values]
-            copies = launch(rounded, phase)
+            copies = started if started and index == 0 else launch(rounded, phase)
             if index < len(besides):
                 besides[index]()
             if narrow:
@@ -247,22 +247,27 @@
 
     held = {}
     for level in (sub, top):
-        plane = []
         place = jnp.int32(0)
-        for step in range(row_span):
-            found = [
-                level_at(step * col_span + offset) == level for offset in range(col_span)
-            ]
-            place = jnp.where(found[0], step, place)
-            plane.append(found)
         known_here = []
-        for bit in range(col_bits + 1):
-            here = jnp.int32(1)
-            for found in plane:
-                for offset in range(1 << bit):
-                    here = jnp.where(found[offset], 0, here)
-            known_here.append(here)
+        here = jnp.int32(1)
+        layers = (0,) if level == sub else (0, layer_size)
+        rounds = [(0, 1)] + [(1 << bit, 2 << bit) for bit in range(col_bits)]
+        for layer in layers:
+            for low, high in rounds if layer == layers[-1] else rounds[:1]:
+                for others in layers if low else (layer,):
+                    for step in range(row_span):
+                        for offset in range(low, high):
+                            found = level_at(others + step * col_span + offset) == level
+                            here = jnp.where(found, 0, here)
+                            if layer == others == low == 0:
+                                place = jnp.where(found, step, place)
+                known_here.append(here)
         held[level] = (place, known_here)
+
+    def reach_of(stream, stage):
+        if stream == TOP_SOLVE:
+            return 1 << stage - 1 if stage else layer_size
+        return 1 << stage
 
     def scatter_rows(source, matrix):
         for step in range(1, row_span):
@@ -289,7 +294,7 @@
             ("double", stream, stage),
             doubled[stream][stage].at[0],
             doubled[stream][stage].at[1],
-            1 << stage if stage < col_bits else layer_size,
+            reach_of(stream, stage),
         )
 
     def gather_rows(stream, stage):
@@ -329,8 +334,6 @@
     for level in range(1, upper_levels + 1):
         pending[level] = pending[level] - jnp.where(my_level == level, rights[OWN], 0.0)
 
-    pl.semaphore_wait(barrier, len(partners))
-
     wide_columns = lax.broadcasted_iota(jnp.int32, (W, W), 1)
     wide_rows = lax.broadcasted_iota(jnp.int32, (W, W), 0)
 
@@ -361,6 +364,31 @@
         return times(large, matrix) + times(small, matrix)
 
     far_is_near = jnp.full((W, W), far_ref[0, OWN], jnp.int32) == 1
+
+    far_product = lower_product(1)
+    fused[0] = half(lower_product(0) + jnp.where(far_is_near, far_product, 0.0))
+    beside_near[0] = fused[0]
+    fused[1] = half(far_product)
+    loads[5].wait()
+    loads[6].wait()
+    fused[2] = half(
+        own_rows(
+            jnp.dot(
+                own_columns(upper_inverse[OWN]),
+                lower_inverse[OWN],
+                preferred_element_type=jnp.float32,
+            )
+        )
+    )
+    far_product = own_rows(upper_product(OWN, 1))
+    far_blocks[0] = half(far_product)
+    near_blocks[0] = half(
+        own_rows(upper_product(OWN, 0)) + jnp.where(far_is_near, far_product, 0.0)
+    )
+    ahead[0] = near_blocks[0]
+    fars[0] = far[OWN][: fars.shape[1], : fars.shape[2]].astype(jnp.float32)
+
+    pl.semaphore_wait(barrier, len(partners))
 
     own_base = [zeros]
     residue = [None]
@@ -382,63 +410,63 @@
 
     leaf_base = [None] * LOCAL_COUNT
 
+    def first_round():
+        scatter_rows(0, fused.at[0])
+        scatter_rows(1, fused.at[2])
+        scatter_rows(2, near_blocks.at[0])
+        hand_ahead(0)
+        hand_out("near", near_blocks.at[0], near_blocks.at[1], 1)
+
+    near_levels = [level_at(offset) for offset in range(NEAR)]
     halves = {}
+
+    def hand_ahead(part):
+        rows = pl.ds(part * (W // 2), W // 2)
+        hand_out(("ahead", part), near_blocks.at[0, rows], ahead.at[1, rows], 2)
+
+    def hand_beside(part):
+        rows = pl.ds(part * (W // 2), W // 2)
+        hand_out(
+            ("beside", part), fused.at[0, rows], beside_near.at[1, rows], col_span
+        )
 
     def beside_up(level):
         if level == 1:
-            far_product = lower_product(1)
-            fused[0] = half(lower_product(0) + jnp.where(far_is_near, far_product, 0.0))
-            beside_near[0] = fused[0]
-            scatter_rows(0, fused.at[0])
-            fused[1] = half(far_product)
-            beside_far[0] = fused[1]
-            loads[5].wait()
-            loads[6].wait()
-            fused[2] = half(
-                own_rows(
-                    jnp.dot(
-                        own_columns(upper_inverse[OWN]),
-                        lower_inverse[OWN],
-                        preferred_element_type=jnp.float32,
-                    )
-                )
-            )
-            scatter_rows(1, fused.at[2])
-            hand_out("beside near", fused.at[0], beside_near.at[1], col_span)
-            far_product = own_rows(upper_product(OWN, 1))
-            far_blocks[0] = half(far_product)
-            near_blocks[0] = half(
-                own_rows(upper_product(OWN, 0)) + jnp.where(far_is_near, far_product, 0.0)
-            )
-            fars[0] = far[OWN][: fars.shape[1], : fars.shape[2]].astype(jnp.float32)
+            first_round()
             return
+        if level == 2:
+            hand_ahead(1)
+        if level == sub - 1:
+            hand_beside(1)
         if level < sub:
-            for stream in (CHAIN, TOP_SOLVE, SUB_SOLVE):
-                double_cols(stream, level - 2)
-            if level == 2:
-                scatter_rows(2, near_blocks.at[0])
             if level > 2:
                 double_cols(BACK, level - 3)
-        if level == sub - 1:
-            hand_out("beside far", fused.at[1], beside_far.at[1], col_span)
-            hand_out("near", near_blocks.at[0], near_blocks.at[1], 1)
+            double_cols(CHAIN, level - 2)
+            if level == 2:
+                double_cols(TOP_SOLVE, 0)
+            double_cols(SUB_SOLVE, level - 2)
+            if level == 2:
+                hand_beside(0)
+            double_cols(TOP_SOLVE, level - 1)
+            if level == sub - 1:
+                double_cols(BACK, level - 2)
         own_solve(level - 1)
         if level == sub:
-            double_cols(TOP_SOLVE, col_bits)
             gather_rows(CHAIN, col_bits)
             gather_rows(SUB_SOLVE, col_bits)
-            double_cols(BACK, col_bits - 1)
-            await_bulk("near")
-            second[0] = near_blocks[pair_place]
-            hand_out("second", second.at[0], second.at[1], 2)
+            gather_rows(TOP_SOLVE, col_bits + 1)
+            gather_rows(BACK, col_bits)
+            await_bulk(("ahead", 0))
+            await_bulk(("ahead", 1))
+            second[0] = ahead[ahead_place]
+            hand_out("second", second.at[0], second.at[1], 1)
             hand_out("far", far_blocks.at[0], far_blocks.at[1], 1)
             hand_out("fars", fars.at[0], fars.at[1], 1)
         if level - 2 < LOCAL_COUNT:
             leaf_products(level - 2)
 
-    near_levels = [level_at(offset) for offset in range(NEAR)]
-    pair_place = jnp.where(near_levels[1] == 2, 1, 0)
-    second_place = jnp.where(near_levels[2] == 2, 1, jnp.where(near_levels[3] == 2, 1, 0))
+    ahead_place = jnp.where(near_levels[2] == 2, 1, 0)
+    second_place = jnp.where(near_levels[1] == 2, 1, jnp.where(near_levels[3] == 2, 1, 0))
 
     def holder(level):
         offset_of = jnp.int32(0)
@@ -448,7 +476,7 @@
 
     for level in range(1, sub):
         if level == sub - 1:
-            for copy, at in launch([half(pending[sub]), half(pending[top])], [col_span]):
+            for copy, at in launch([half(pending[sub])], [col_span]):
                 halves["copy"], halves["at"] = copy, at
         gathered = exchange(
             [pending[level]], plans[level - 1], False, [functools.partial(beside_up, level)]
@@ -465,24 +493,26 @@
     on_side = jnp.where(across == sub - 1, 1, 0)
     here = spread(jnp.where(my_level_scalar == sub - 1, 1, on_side)) == 1
     halves["copy"].wait_recv()
-    await_bulk("beside near")
-    await_bulk("beside far")
-    products = [
-        times(residue[0], beside_near[on_side]),
-        times(residue[0], beside_far[on_side]),
-    ]
-    values = [
-        pending[level]
-        + incoming[halves["at"] + index].astype(jnp.float32)
-        + jnp.where(here, products[index], 0.0)
-        for index, level in enumerate((sub, top))
-    ]
-    sums = exchange(values, plans[sub - 1], False, [functools.partial(beside_up, sub)])
-    gather_rows(TOP_SOLVE, col_bits + 1)
-    gather_rows(BACK, col_bits)
+    far_up(sub - 1)
+    await_bulk(("beside", 0))
+    await_bulk(("beside", 1))
+    product = times(residue[0], beside_near[on_side])
+    value = (
+        pending[sub]
+        + incoming[halves["at"]].astype(jnp.float32)
+        + jnp.where(here, product, 0.0)
+    )
+    layer_plan = down_plans[-1]
+
+    def beside_sub():
+        halves["layer"] = launch([half(pending[top])], layer_plan[0])
+        beside_up(sub)
+
+    sums = exchange([value], plans[sub - 1], False, [beside_sub])
     sub_residue = half(-sums[0])
     await_spread(("gather", CHAIN))
-    layer_sum = sums[1] + times(sub_residue, whole[CHAIN][...])
+    chained = times(sub_residue, whole[CHAIN][...])
+    layer_sum = exchange([pending[top]], layer_plan, False, [], halves["layer"])[0] + chained
     sub_base = [None]
 
     def beside_top():
@@ -584,12 +614,13 @@
     plans.append(exchange_plan([sub]))
     down_plans = [[]] * NEAR_BITS
     down_plans += [exchange_plan(list(range(level))) for level in range(NEAR_BITS + 1, sub)]
-    vectors = [1] * (sub - 1) + [2, 1, 2] + [1] * len(down_plans)
+    down_plans.append(exchange_plan(list(range(sub))))
+    vectors = [1] * (sub + 2 + len(down_plans))
     routes = list(zip(vectors, plans + [[[col_span]]] + down_plans))
     phases = sum(amount * len(plan) for amount, plan in routes)
     messages = sum(len(phase) for _, plan in routes for phase in plan)
     boxes = sum(amount * len(phase) for amount, plan in routes for phase in plan)
-    handed = 6 + NEAR - 1
+    handed = 8 + NEAR - 1
     streams, sources = len(SOURCES), len(set(SOURCES.values()))
     strip = W // row_span
     spread_count = (sources + streams) * (row_span - 1) + streams * col_bits + 1

time: 41.9 us -> 40 us (0.955)
  Pallas kernels: 40.2 us -> 38.3 us
    pallas_call x1, Pallas kernels: 40.2 us -> 38.3 us  [local(): pl.pallas_call(functools.partial(kernel, spans, plans, down_plans), out_s...]
where the time goes in v3:
time: 40 us; the launch traced here: 39.8 us
  Pallas kernels  38.3 us (96%)
  local copies, waits for them, and re-layouts  1.47 us (4%)
    pallas_call x1, Pallas kernels, local(): pl.pallas_call(functools.partial(kernel, spans, plans, down_plans), out_s...  38.3 us
    unnamed x1, local copies, waits for them, and re-layouts  1.47 us

profile of v3, /device:TPU:0, one launch (start us, length us, event | category | flops | bytes accessed | tf_op | source)
XLA Modules:
  0.0 39.8 jit_solution(8495491575341181018)
XLA Ops:
  0.0 38.3 %tree_solve.1 = f32[1,4,16,256]{3,2,1,0:T(8,128)} custom-call(f32[1,4,16,256]{3,2,1,0:T(8,128)} %rights_hbm.1, bf16[1,4,256,256]{3,2,1,0:T(8,128)(2,1)} %lower_inverse_hbm.1, bf16[1,4,256,256]{3,2,1,0:T(8,128)(2,1)} %upper_inverse_hbm.1, bf16[1,4,2,256,256]{4,3,2,1,0:T(8,128)(2,1)} %lower_blocks_hbm.1, bf16[1,4,2,256,256]{4,3,2,1,0:T(8,128)(2,1)} %upper_blocks_hbm.1, ...), custom_call_target="tpu_custom_call" | custom-call | tf_op jit(solution)/shard_map/tree_solve/pallas_call | solution.py:629
  38.3 1.5 %copy.10 = f32[1,4,16,256]{3,2,1,0:T(8,128)} copy(f32[1,4,16,256]{3,2,1,0:T(8,128)} %tree_solve.1) | data formatting | bytes 131072

commit v4 on v3

--- a/solution.py
+++ b/solution.py
@@ -64,7 +64,7 @@
     widths_ref,
     far_ref,
     owner_ref,
-    out_ref,
+    out_hbm,
     rights,
     lower_inverse,
     upper_inverse,
@@ -83,7 +83,9 @@
     scattered,
     doubled,
     whole,
+    solved_slots,
     load_sems,
+    store_sems,
     send_sems,
     recv_sems,
     bulk_send_sems,
@@ -161,30 +163,62 @@
     counts = [0, 0, 0]
     sends = []
 
+    class Joined:
+        def __init__(self, target, send_sem, recv_sem):
+            self.sent = pltpu.make_async_copy(target, target, send_sem)
+            self.arrived = pltpu.make_async_copy(target, target, recv_sem)
+
+        def wait_recv(self):
+            self.arrived.wait()
+
+        def wait_send(self):
+            self.sent.wait()
+
     def launch(rounded, phase):
         outbox, amount = counts[0], len(rounded)
         counts[0] += amount
         for index, part in enumerate(rounded):
             outgoing[outbox + index] = part
-        copies = []
-        for offset in phase:
-            at, message = counts[1], counts[2]
-            counts[1] += amount
-            counts[2] += 1
-            copy = pltpu.make_async_remote_copy(
+        begin, message = counts[1], counts[2]
+        counts[1] += amount * len(phase)
+        counts[2] += 1
+        for index, offset in enumerate(phase):
+            pltpu.make_async_remote_copy(
                 src_ref=outgoing.at[pl.ds(outbox, amount)],
-                dst_ref=incoming.at[pl.ds(at, amount)],
+                dst_ref=incoming.at[pl.ds(begin + index * amount, amount)],
                 send_sem=send_sems.at[message],
                 recv_sem=recv_sems.at[message],
                 device_id=peer(offset),
                 device_id_type=pl.DeviceIdType.MESH,
-            )
-            copy.start()
-            copies.append((copy, at))
-        sends.extend(copies)
+            ).start()
+        copy = Joined(
+            incoming.at[pl.ds(begin, amount * len(phase))],
+            send_sems.at[message],
+            recv_sems.at[message],
+        )
+        copies = [(copy, begin + index * amount) for index in range(len(phase))]
+        sends.append(copies[0])
         return copies
 
     bulk = {}
+    drained = set()
+    spreads = []
+
+    def drain():
+        copies = [copy for copy, _ in sends] + list(bulk.values()) + spreads
+        for copy in copies:
+            if id(copy) not in drained:
+                drained.add(id(copy))
+                copy.wait_send()
+
+    stores = []
+
+    def store_out(slots):
+        store = pltpu.make_async_copy(
+            solved_slots.at[slots], out_hbm.at[0, slots], store_sems.at[len(stores)]
+        )
+        store.start()
+        stores.append(store)
 
     def hand_out(name, source, target, offset):
         at = len(bulk)
@@ -213,8 +247,8 @@
                 besides[index]()
             if narrow:
                 values = [part.astype(jnp.float32) for part in rounded]
-            for copy, at in copies:
-                copy.wait_recv()
+            copies[0][0].wait_recv()
+            for _, at in copies:
                 values = [
                     value + incoming[at + part].astype(jnp.float32)
                     for part, value in enumerate(values)
@@ -224,22 +258,22 @@
     strip = W // row_span
     my_strip = pl.ds(pl.multiple_of(row_at * strip, strip), strip)
     stream_level = {CHAIN: sub, TOP_SOLVE: top, SUB_SOLVE: sub, BACK: sub}
-    spreads = []
     spread_waits = {}
 
-    def spread_copy(key, source, target, offset):
+    def spread_copies(key, pairs, extent):
         at = len(spreads)
-        copy = pltpu.make_async_remote_copy(
-            src_ref=source,
-            dst_ref=target,
-            send_sem=spread_send_sems.at[at],
-            recv_sem=spread_recv_sems.at[at],
-            device_id=peer(offset),
-            device_id_type=pl.DeviceIdType.MESH,
-        )
-        copy.start()
+        for source, target, offset in pairs:
+            pltpu.make_async_remote_copy(
+                src_ref=source,
+                dst_ref=target,
+                send_sem=spread_send_sems.at[at],
+                recv_sem=spread_recv_sems.at[at],
+                device_id=peer(offset),
+                device_id_type=pl.DeviceIdType.MESH,
+            ).start()
+        copy = Joined(extent, spread_send_sems.at[at], spread_recv_sems.at[at])
         spreads.append(copy)
-        spread_waits.setdefault(key, []).append(copy)
+        spread_waits[key] = [copy]
 
     def await_spread(key):
         for copy in spread_waits.pop(key, ()):
@@ -269,15 +303,15 @@
             return 1 << stage - 1 if stage else layer_size
         return 1 << stage
 
+    others = pl.ds(1, row_span - 1)
+
     def scatter_rows(source, matrix):
+        pairs = []
         for step in range(1, row_span):
             start = pl.multiple_of(flip_bits(row_at, step) * strip, strip)
-            spread_copy(
-                ("scatter", source),
-                matrix.at[pl.ds(start, strip)],
-                scattered[source].at[step],
-                step * col_span,
-            )
+            rows = matrix.at[pl.ds(start, strip)]
+            pairs.append((rows, scattered[source].at[step], step * col_span))
+        spread_copies(("scatter", source), pairs, scattered[source].at[others])
         scattered[source][0] = matrix[my_strip]
 
     def merged(stream, stage):
@@ -289,23 +323,17 @@
         return doubled[stream][stage - 1][known_here[stage - 1]]
 
     def double_cols(stream, stage):
+        mine, theirs = (doubled[stream][stage].at[side] for side in range(2))
         doubled[stream][stage][0] = merged(stream, stage)
-        spread_copy(
-            ("double", stream, stage),
-            doubled[stream][stage].at[0],
-            doubled[stream][stage].at[1],
-            reach_of(stream, stage),
-        )
+        pairs = [(mine, theirs, reach_of(stream, stage))]
+        spread_copies(("double", stream, stage), pairs, theirs)
 
     def gather_rows(stream, stage):
         whole[stream][my_strip] = merged(stream, stage)
-        for step in range(1, row_span):
-            spread_copy(
-                ("gather", stream),
-                whole[stream].at[my_strip],
-                whole[stream].at[my_strip],
-                step * col_span,
-            )
+        rows = whole[stream].at[my_strip]
+        pairs = [(rows, rows, step * col_span) for step in range(1, row_span)]
+        extent = whole[stream].at[pl.ds(0, strip * (row_span - 1))]
+        spread_copies(("gather", stream), pairs, extent)
 
     pending = [None] + [zeros for _ in range(upper_levels)]
 
@@ -407,6 +435,18 @@
     def leaf_products(slot):
         for block_id in range(NB):
             fused[3 + 2 * slot + block_id] = half(upper_product(slot, block_id))
+        if slot == 2:
+            kept = half(
+                jnp.where(
+                    wide_rows < widths_ref[0, 2], fused[3 + 2 * 2].astype(jnp.float32), 0.0
+                )
+            )
+            for leaf in range(2):
+                fused[9 + leaf] = half(
+                    jnp.dot(
+                        fused[3 + 2 * leaf], kept, preferred_element_type=jnp.float32
+                    )
+                )
 
     leaf_base = [None] * LOCAL_COUNT
 
@@ -540,6 +580,7 @@
     own_solution = own_solution + jnp.where(my_level == sub, solved, 0.0)
     known[sub] = half(solved).astype(jnp.float32)
 
+    marks = [len(sends), len(bulk), len(spreads)]
     for level in range(sub - 1, NEAR_BITS, -1):
         chosen = zeros
         for target in range(level + 1, upper_levels + 1):
@@ -554,6 +595,15 @@
                 bases[0] = half(jnp.where(my_level == 1, own_base[0], base))
                 for offset in range(1, NEAR):
                     hand_out(("base", offset), bases.at[0], bases.at[offset], offset)
+                for name in bulk:
+                    if name[0] != "base":
+                        await_bulk(name)
+            copies = [copy for copy, _ in sends[: marks[0]]]
+            copies += list(bulk.values())[: marks[1]] + spreads[: marks[2]]
+            for copy in copies:
+                if id(copy) not in drained:
+                    drained.add(id(copy))
+                    copy.wait_send()
 
         known[level] = exchange([solved], down_plans[level - 1], True, [beside_down])[0]
     for name in bulk:
@@ -575,23 +625,22 @@
     solved = base - times(half(solved), near_blocks[at])
     own_solution = own_solution + jnp.where(my_level == 1, solved, 0.0)
     known[1] = half(solved).astype(jnp.float32)
-    leaf_base[2] = leaf_base[2] - times(pick(2, 0, 2), fused[3 + 2 * 2 + 1])
-    out_ref[0, OWN] = own_solution
-
+    solved_slots[OWN] = own_solution
+    store_out(pl.ds(OWN, 1))
     nearest = half(known[1])
-    root = padded(2, leaf_base[2] - times(nearest, fused[3 + 2 * 2]))
-    out_ref[0, 2] = root
+    root_base = leaf_base[2] - times(pick(2, 0, 2), fused[3 + 2 * 2 + 1])
+    solved_slots[2] = padded(2, root_base - times(nearest, fused[3 + 2 * 2]))
+    store_out(pl.ds(2, 1))
+    root_part = half(padded(2, root_base))
     for slot in range(2):
         solved = leaf_base[slot] - times(pick(slot, -1, 1), fused[3 + 2 * slot + 1])
-        solved = solved - times(half(root), fused[3 + 2 * slot])
-        out_ref[0, slot] = padded(slot, solved)
-
-    for copy, _ in sends:
-        copy.wait_send()
-    for copy in bulk.values():
-        copy.wait_send()
-    for copy in spreads:
-        copy.wait_send()
+        solved = solved - times(root_part, fused[3 + 2 * slot])
+        solved_slots[slot] = padded(slot, solved + times(nearest, fused[9 + slot]))
+
+    store_out(pl.ds(0, 2))
+    drain()
+    for store in stores:
+        store.wait()
 
 
 def local(
@@ -618,19 +667,19 @@
     vectors = [1] * (sub + 2 + len(down_plans))
     routes = list(zip(vectors, plans + [[[col_span]]] + down_plans))
     phases = sum(amount * len(plan) for amount, plan in routes)
-    messages = sum(len(phase) for _, plan in routes for phase in plan)
+    messages = sum(len(plan) for _, plan in routes)
     boxes = sum(amount * len(phase) for amount, plan in routes for phase in plan)
     handed = 8 + NEAR - 1
     streams, sources = len(SOURCES), len(set(SOURCES.values()))
     strip = W // row_span
-    spread_count = (sources + streams) * (row_span - 1) + streams * col_bits + 1
+    spread_count = sources + streams * (col_bits + 1) + 1
     hbm = pl.BlockSpec(memory_space=pl.ANY)
     smem = pl.BlockSpec(memory_space=pltpu.SMEM)
     return pl.pallas_call(
         functools.partial(kernel, spans, plans, down_plans),
         out_shape=jax.ShapeDtypeStruct(right_sides.shape, jnp.float32),
         in_specs=[hbm] * 5 + [smem] * 3,
-        out_specs=pl.BlockSpec(memory_space=pltpu.VMEM),
+        out_specs=hbm,
         scratch_shapes=[
             pltpu.VMEM(right_sides.shape[1:], jnp.float32),
             pltpu.VMEM(lower_inverse.shape[1:], jnp.bfloat16),
@@ -639,7 +688,7 @@
             pltpu.VMEM(upper_blocks.shape[1:], jnp.bfloat16),
             pltpu.VMEM((phases, RHS, W), jnp.bfloat16),
             pltpu.VMEM((boxes, RHS, W), jnp.bfloat16),
-            pltpu.VMEM((3 + NB * LOCAL_COUNT, W, W), jnp.bfloat16),
+            pltpu.VMEM((5 + NB * LOCAL_COUNT, W, W), jnp.bfloat16),
             pltpu.VMEM((2, W, W), jnp.bfloat16),
             pltpu.VMEM((2, W, W), jnp.bfloat16),
             pltpu.VMEM((2, W, W), jnp.bfloat16),
@@ -650,7 +699,9 @@
             [pltpu.VMEM((row_span, strip, W), jnp.bfloat16)] * sources,
             [[pltpu.VMEM((2, strip, W), jnp.bfloat16)] * (col_bits + 1)] * streams,
             [pltpu.VMEM((W, W), jnp.bfloat16)] * streams,
+            pltpu.VMEM(right_sides.shape[1:], jnp.float32),
             pltpu.SemaphoreType.DMA((7,)),
+            pltpu.SemaphoreType.DMA((3,)),
             pltpu.SemaphoreType.DMA((messages,)),
             pltpu.SemaphoreType.DMA((messages,)),
             pltpu.SemaphoreType.DMA((handed,)),

time: 40 us -> 39 us (0.975)
  Pallas kernels: 38.3 us -> 37.3 us
    pallas_call x1, Pallas kernels: 38.3 us -> 37.3 us  [local(): pl.pallas_call(functools.partial(kernel, spans, plans, down_plans), out_s...]
where the time goes in v4:
time: 39 us; the launch traced here: 38.8 us
  Pallas kernels  37.3 us (96%)
  local copies, waits for them, and re-layouts  1.47 us (4%)
    pallas_call x1, Pallas kernels, local(): pl.pallas_call(functools.partial(kernel, spans, plans, down_plans), out_s...  37.3 us
    unnamed x1, local copies, waits for them, and re-layouts  1.47 us

profile of v4, /device:TPU:0, one launch (start us, length us, event | category | flops | bytes accessed | tf_op | source)
XLA Modules:
  0.0 38.8 jit_solution(3253709385484711252)
XLA Ops:
  0.0 37.3 %tree_solve.1 = f32[1,4,16,256]{3,2,1,0:T(8,128)} custom-call(f32[1,4,16,256]{3,2,1,0:T(8,128)} %rights_hbm.1, bf16[1,4,256,256]{3,2,1,0:T(8,128)(2,1)} %lower_inverse_hbm.1, bf16[1,4,256,256]{3,2,1,0:T(8,128)(2,1)} %upper_inverse_hbm.1, bf16[1,4,2,256,256]{4,3,2,1,0:T(8,128)(2,1)} %lower_blocks_hbm.1, bf16[1,4,2,256,256]{4,3,2,1,0:T(8,128)(2,1)} %upper_blocks_hbm.1, ...), custom_call_target="tpu_custom_call" | custom-call | tf_op jit(solution)/shard_map/tree_solve/pallas_call | solution.py:678
  37.3 1.5 %copy.10 = f32[1,4,16,256]{3,2,1,0:T(8,128)} copy(f32[1,4,16,256]{3,2,1,0:T(8,128)} %tree_solve.1) | data formatting | bytes 131072

commit v5 on v4

--- a/solution.py
+++ b/solution.py
@@ -84,6 +84,7 @@
     doubled,
     whole,
     solved_slots,
+    sent_strips,
     load_sems,
     store_sems,
     send_sems,
@@ -112,10 +113,8 @@
 
     pieces = [
         (rights_hbm.at[0], rights),
-        (lower_inverse_hbm.at[0, pl.ds(0, 2)], lower_inverse.at[pl.ds(0, 2)]),
-        (lower_blocks_hbm.at[0, pl.ds(0, 2)], lower_blocks.at[pl.ds(0, 2)]),
-        (lower_inverse_hbm.at[0, pl.ds(2, 2)], lower_inverse.at[pl.ds(2, 2)]),
-        (lower_blocks_hbm.at[0, pl.ds(2, 2)], lower_blocks.at[pl.ds(2, 2)]),
+        (lower_inverse_hbm.at[0], lower_inverse),
+        (lower_blocks_hbm.at[0], lower_blocks),
         (upper_blocks_hbm.at[0], upper_blocks),
         (upper_inverse_hbm.at[0], upper_inverse),
     ]
@@ -186,14 +185,14 @@
             pltpu.make_async_remote_copy(
                 src_ref=outgoing.at[pl.ds(outbox, amount)],
                 dst_ref=incoming.at[pl.ds(begin + index * amount, amount)],
-                send_sem=send_sems.at[message],
+                send_sem=send_sems.at[0],
                 recv_sem=recv_sems.at[message],
                 device_id=peer(offset),
                 device_id_type=pl.DeviceIdType.MESH,
             ).start()
         copy = Joined(
             incoming.at[pl.ds(begin, amount * len(phase))],
-            send_sems.at[message],
+            send_sems.at[0],
             recv_sems.at[message],
         )
         copies = [(copy, begin + index * amount) for index in range(len(phase))]
@@ -201,15 +200,15 @@
         return copies
 
     bulk = {}
-    drained = set()
     spreads = []
+    strips_sent = [0]
+    vectors_sent = [0]
 
     def drain():
-        copies = [copy for copy, _ in sends] + list(bulk.values()) + spreads
-        for copy in copies:
-            if id(copy) not in drained:
-                drained.add(id(copy))
-                copy.wait_send()
+        for copy in bulk.values():
+            copy.wait_send()
+        pltpu.make_async_copy(incoming, incoming, send_sems.at[0]).wait()
+        pltpu.make_async_copy(sent_strips, sent_strips, spread_send_sems.at[0]).wait()
 
     stores = []
 
@@ -266,12 +265,13 @@
             pltpu.make_async_remote_copy(
                 src_ref=source,
                 dst_ref=target,
-                send_sem=spread_send_sems.at[at],
+                send_sem=spread_send_sems.at[0],
                 recv_sem=spread_recv_sems.at[at],
                 device_id=peer(offset),
                 device_id_type=pl.DeviceIdType.MESH,
             ).start()
-        copy = Joined(extent, spread_send_sems.at[at], spread_recv_sems.at[at])
+        strips_sent[0] += len(pairs)
+        copy = Joined(extent, spread_send_sems.at[0], spread_recv_sems.at[at])
         spreads.append(copy)
         spread_waits[key] = [copy]
 
@@ -354,8 +354,6 @@
     )
     for slot in range(2):
         scatter_up(times(half(forward[slot]), lower_blocks[slot, 1]), slot, 0)
-    loads[3].wait()
-    loads[4].wait()
     forward[2] = padded(2, times(half(rights[2] - near), lower_inverse[2]))
     pending[1] = pending[1] + times(half(forward[2]), lower_blocks[2, 0])
     scatter_up(times(half(forward[2]), lower_blocks[2, 1]), 2, 1)
@@ -397,8 +395,8 @@
     fused[0] = half(lower_product(0) + jnp.where(far_is_near, far_product, 0.0))
     beside_near[0] = fused[0]
     fused[1] = half(far_product)
-    loads[5].wait()
-    loads[6].wait()
+    loads[3].wait()
+    loads[4].wait()
     fused[2] = half(
         own_rows(
             jnp.dot(
@@ -479,9 +477,9 @@
         if level == sub - 1:
             hand_beside(1)
         if level < sub:
+            double_cols(CHAIN, level - 2)
             if level > 2:
                 double_cols(BACK, level - 3)
-            double_cols(CHAIN, level - 2)
             if level == 2:
                 double_cols(TOP_SOLVE, 0)
             double_cols(SUB_SOLVE, level - 2)
@@ -580,7 +578,6 @@
     own_solution = own_solution + jnp.where(my_level == sub, solved, 0.0)
     known[sub] = half(solved).astype(jnp.float32)
 
-    marks = [len(sends), len(bulk), len(spreads)]
     for level in range(sub - 1, NEAR_BITS, -1):
         chosen = zeros
         for target in range(level + 1, upper_levels + 1):
@@ -598,12 +595,6 @@
                 for name in bulk:
                     if name[0] != "base":
                         await_bulk(name)
-            copies = [copy for copy, _ in sends[: marks[0]]]
-            copies += list(bulk.values())[: marks[1]] + spreads[: marks[2]]
-            for copy in copies:
-                if id(copy) not in drained:
-                    drained.add(id(copy))
-                    copy.wait_send()
 
         known[level] = exchange([solved], down_plans[level - 1], True, [beside_down])[0]
     for name in bulk:
@@ -630,14 +621,13 @@
     nearest = half(known[1])
     root_base = leaf_base[2] - times(pick(2, 0, 2), fused[3 + 2 * 2 + 1])
     solved_slots[2] = padded(2, root_base - times(nearest, fused[3 + 2 * 2]))
-    store_out(pl.ds(2, 1))
     root_part = half(padded(2, root_base))
     for slot in range(2):
         solved = leaf_base[slot] - times(pick(slot, -1, 1), fused[3 + 2 * slot + 1])
         solved = solved - times(root_part, fused[3 + 2 * slot])
         solved_slots[slot] = padded(slot, solved + times(nearest, fused[9 + slot]))
 
-    store_out(pl.ds(0, 2))
+    store_out(pl.ds(0, 3))
     drain()
     for store in stores:
         store.wait()
@@ -672,6 +662,7 @@
     handed = 8 + NEAR - 1
     streams, sources = len(SOURCES), len(set(SOURCES.values()))
     strip = W // row_span
+    strips = (sources + streams) * (row_span - 1) + streams * col_bits + 1
     spread_count = sources + streams * (col_bits + 1) + 1
     hbm = pl.BlockSpec(memory_space=pl.ANY)
     smem = pl.BlockSpec(memory_space=pltpu.SMEM)
@@ -700,13 +691,14 @@
             [[pltpu.VMEM((2, strip, W), jnp.bfloat16)] * (col_bits + 1)] * streams,
             [pltpu.VMEM((W, W), jnp.bfloat16)] * streams,
             pltpu.VMEM(right_sides.shape[1:], jnp.float32),
-            pltpu.SemaphoreType.DMA((7,)),
-            pltpu.SemaphoreType.DMA((3,)),
-            pltpu.SemaphoreType.DMA((messages,)),
+            pltpu.VMEM((strips, strip, W), jnp.bfloat16),
+            pltpu.SemaphoreType.DMA((5,)),
+            pltpu.SemaphoreType.DMA((2,)),
+            pltpu.SemaphoreType.DMA((1,)),
             pltpu.SemaphoreType.DMA((messages,)),
             pltpu.SemaphoreType.DMA((handed,)),
             pltpu.SemaphoreType.DMA((handed,)),
-            pltpu.SemaphoreType.DMA((spread_count,)),
+            pltpu.SemaphoreType.DMA((1,)),
             pltpu.SemaphoreType.DMA((spread_count,)),
         ],
         compiler_params=pltpu.CompilerParams(collective_id=0, has_side_effects=True),

time: 39 us -> 38.7 us (level)
  no operation moved by 1% of the time
where the time goes in v5:
time: 38.7 us; the launch traced here: 38.6 us
  Pallas kernels  37.1 us (96%)
  local copies, waits for them, and re-layouts  1.47 us (4%)
    pallas_call x1, Pallas kernels, local(): pl.pallas_call(functools.partial(kernel, spans, plans, down_plans), out_s...  37.1 us
    unnamed x1, local copies, waits for them, and re-layouts  1.47 us

profile of v5, /device:TPU:0, one launch (start us, length us, event | category | flops | bytes accessed | tf_op | source)
XLA Modules:
  0.0 38.6 jit_solution(8215649803420575291)
XLA Ops:
  0.0 37.1 %tree_solve.1 = f32[1,4,16,256]{3,2,1,0:T(8,128)} custom-call(f32[1,4,16,256]{3,2,1,0:T(8,128)} %rights_hbm.1, bf16[1,4,256,256]{3,2,1,0:T(8,128)(2,1)} %lower_inverse_hbm.1, bf16[1,4,256,256]{3,2,1,0:T(8,128)(2,1)} %upper_inverse_hbm.1, bf16[1,4,2,256,256]{4,3,2,1,0:T(8,128)(2,1)} %lower_blocks_hbm.1, bf16[1,4,2,256,256]{4,3,2,1,0:T(8,128)(2,1)} %upper_blocks_hbm.1, ...), custom_call_target="tpu_custom_call" | custom-call | tf_op jit(solution)/shard_map/tree_solve/pallas_call | solution.py:669
  37.1 1.5 %copy.10 = f32[1,4,16,256]{3,2,1,0:T(8,128)} copy(f32[1,4,16,256]{3,2,1,0:T(8,128)} %tree_solve.1) | data formatting | bytes 131072

commit v6 on v5

--- a/solution.py
+++ b/solution.py
@@ -204,9 +204,19 @@
     strips_sent = [0]
     vectors_sent = [0]
 
+    groups = ["near", "second", "far", "ahead", "beside", "fars", "base"]
+    joint = {
+        "ahead": ahead.at[1],
+        "beside": beside_near.at[1],
+        "base": bases.at[pl.ds(1, NEAR - 1)],
+    }
+
     def drain():
-        for copy in bulk.values():
-            copy.wait_send()
+        blocks = fused.at[pl.ds(0, 5)]
+        vectors = bases.at[pl.ds(1, NEAR - 1)]
+        pltpu.make_async_copy(blocks, blocks, bulk_send_sems.at[0]).wait()
+        pltpu.make_async_copy(fars.at[1], fars.at[1], bulk_send_sems.at[1]).wait()
+        pltpu.make_async_copy(vectors, vectors, bulk_send_sems.at[2]).wait()
         pltpu.make_async_copy(incoming, incoming, send_sems.at[0]).wait()
         pltpu.make_async_copy(sent_strips, sent_strips, spread_send_sems.at[0]).wait()
 
@@ -220,23 +230,26 @@
         stores.append(store)
 
     def hand_out(name, source, target, offset):
-        at = len(bulk)
-        bulk[name] = pltpu.make_async_remote_copy(
+        group = name if isinstance(name, str) else name[0]
+        at = groups.index(group)
+        pltpu.make_async_remote_copy(
             src_ref=source,
             dst_ref=target,
-            send_sem=bulk_send_sems.at[at],
+            send_sem=bulk_send_sems.at[max(at - 4, 0)],
             recv_sem=bulk_recv_sems.at[at],
             device_id=peer(offset),
             device_id_type=pl.DeviceIdType.MESH,
-        )
-        bulk[name].start()
+        ).start()
+        extent = joint.get(group, target)
+        bulk[name] = pltpu.make_async_copy(extent, extent, bulk_recv_sems.at[at])
 
     received = set()
 
     def await_bulk(name):
-        if name not in received:
-            received.add(name)
-            bulk[name].wait_recv()
+        group = name if isinstance(name, str) else name[0]
+        if group not in received:
+            received.add(group)
+            bulk[name].wait()
 
     def exchange(values, plan, narrow, besides, started=None):
         for index, phase in enumerate(plan):
@@ -659,7 +672,6 @@
     phases = sum(amount * len(plan) for amount, plan in routes)
     messages = sum(len(plan) for _, plan in routes)
     boxes = sum(amount * len(phase) for amount, plan in routes for phase in plan)
-    handed = 8 + NEAR - 1
     streams, sources = len(SOURCES), len(set(SOURCES.values()))
     strip = W // row_span
     strips = (sources + streams) * (row_span - 1) + streams * col_bits + 1
@@ -696,8 +708,8 @@
             pltpu.SemaphoreType.DMA((2,)),
             pltpu.SemaphoreType.DMA((1,)),
             pltpu.SemaphoreType.DMA((messages,)),
-            pltpu.SemaphoreType.DMA((handed,)),
-            pltpu.SemaphoreType.DMA((handed,)),
+            pltpu.SemaphoreType.DMA((3,)),
+            pltpu.SemaphoreType.DMA((7,)),
             pltpu.SemaphoreType.DMA((1,)),
             pltpu.SemaphoreType.DMA((spread_count,)),
         ],

time: 38.7 us -> 38.6 us (level)
  no operation moved by 1% of the time
where the time goes in v6:
time: 38.6 us; the launch traced here: 38.5 us
  Pallas kernels  37 us (96%)
  local copies, waits for them, and re-layouts  1.47 us (4%)
    pallas_call x1, Pallas kernels, local(): pl.pallas_call(functools.partial(kernel, spans, plans, down_plans), out_s...  37 us
    unnamed x1, local copies, waits for them, and re-layouts  1.47 us

profile of v6, /device:TPU:0, one launch (start us, length us, event | category | flops | bytes accessed | tf_op | source)
XLA Modules:
  0.0 38.5 jit_solution(7517583631115289813)
XLA Ops:
  0.0 37.0 %tree_solve.1 = f32[1,4,16,256]{3,2,1,0:T(8,128)} custom-call(f32[1,4,16,256]{3,2,1,0:T(8,128)} %rights_hbm.1, bf16[1,4,256,256]{3,2,1,0:T(8,128)(2,1)} %lower_inverse_hbm.1, bf16[1,4,256,256]{3,2,1,0:T(8,128)(2,1)} %upper_inverse_hbm.1, bf16[1,4,2,256,256]{4,3,2,1,0:T(8,128)(2,1)} %lower_blocks_hbm.1, bf16[1,4,2,256,256]{4,3,2,1,0:T(8,128)(2,1)} %upper_blocks_hbm.1, ...), custom_call_target="tpu_custom_call" | custom-call | tf_op jit(solution)/shard_map/tree_solve/pallas_call | solution.py:681
  37.0 1.5 %copy.10 = f32[1,4,16,256]{3,2,1,0:T(8,128)} copy(f32[1,4,16,256]{3,2,1,0:T(8,128)} %tree_solve.1) | data formatting | bytes 131072
